TPU v7x, 256 devices: a whole 4x4x8 slice. The times are simulated.
256 devices in a mesh: dp: 32 (over z, y), mp: 8 (over x, core).
Axes of the slice: x: 4, y: 4, z: 8, core: 2. Of those that a mesh axis runs over, the one named last changes fastest.
Arguments:
- queries: bfloat16 [4096, 8192], P('dp', 'mp'), may hold values from -8 to 8
- tree_keys: bfloat16 [4096, 1024], P('dp', 'mp'), may hold values from -18 to 18
- tree_values: bfloat16 [4096, 1024], P('dp', 'mp'), may hold values from -6 to 6
- cache_keys: bfloat16 [64, 4096, 1024], P('dp', None, 'mp'), may hold values from -8 to 8
- cache_values: bfloat16 [64, 4096, 1024], P('dp', None, 'mp'), may hold values from -6 to 6
- cache_lens: int32 [64], P('dp'), may hold values from 1024 to 4096, as said below
- parents: int32 [64, 64], P('dp'), may hold values from -1 to 62, as said below
- accepted_nodes: int32 [64, 8], P('dp'), may hold values from 0 to 63, as said below
- residual: bfloat16 [4096, 8192], P('dp', 'mp'), may hold values from -1.796875 to 1.796875
- out_weight: bfloat16 [8192, 8192], P('mp', 'dp'), may hold values from -0.0625 to 0.0625
Outputs:
- tree_hidden: bfloat16 [4096, 8192], P('dp', 'mp')
- accepted_hidden: bfloat16 [512, 8192], P(None, 'mp')
Inputs may be any that keep to these rules, and one draw needn't show every extreme that they name: parents[r, 0] = -1 and 0 <= parents[r, i] < i for i >= 1. accepted_nodes[r, 0] = 0, the nodes of a row increase, and parents[r, accepted_nodes[r, a + 1]] = accepted_nodes[r, a]. `cache_lens`: some request has exactly 4096 filled positions.
All inputs are finite; a program needn't handle non-finite values.
Results may differ from a plain program's by a relative error of at most 0.015.
Values may be sent and summed in bfloat16 or wider, within the bound.
No kernel may reach another device: no remote copies, remote signals or barrier semaphores. Data moves between devices by JAX's collectives and lax.ppermute only.
A program may use at most 64 MiB of HBM per device.

v0:
```python
import math

import jax
import jax.numpy as jnp
from jax import lax
from jax.experimental import pallas as pl
from jax.experimental.pallas import tpu as pltpu
from jax.sharding import PartitionSpec as P

HEADS = 64
KV_HEADS = 8
HD = 128
GROUP = HEADS // KV_HEADS
Z, Y, X, C = 8, 4, 4, 2
KEY_BLOCK = 512
neg_large = -1e30


def attention_kernel(
    lens_ref, parents_ref, q_ref, tk_ref, tv_ref, k_ref, v_ref, out_ref, scores, maxes
):
    request = pl.program_id(0)
    nodes = q_ref.shape[0]
    rows = nodes * GROUP
    scale = 1.0 / math.sqrt(HD)
    length = lens_ref[request]

    parents = parents_ref[0]
    col = lax.broadcasted_iota(jnp.int32, (nodes, nodes), 1)
    row = lax.broadcasted_iota(jnp.int32, (nodes, nodes), 0)
    reached = ((parents == col) | (row == col)).astype(jnp.bfloat16)
    for _ in range((nodes - 1).bit_length()):
        squared = jnp.dot(reached, reached, preferred_element_type=jnp.float32)
        reached = jnp.minimum(squared, 1.0).astype(jnp.bfloat16)
    ancestor = reached.astype(jnp.float32) > 0.5

    queries = jnp.concatenate([q_ref[:, g * HD : (g + 1) * HD] for g in range(GROUP)], axis=0)
    dims = (((1,), (1,)), ((), ()))
    tree = lax.dot_general(queries, tk_ref[...], dims, preferred_element_type=jnp.float32) * scale
    tree = jnp.where(jnp.concatenate([ancestor] * GROUP, axis=0), tree, neg_large)
    maxes[...] = jnp.full(maxes.shape, neg_large, jnp.float32)
    blocks = (length + KEY_BLOCK - 1) // KEY_BLOCK

    def score(b, carry):
        start = pl.multiple_of(b * KEY_BLOCK, KEY_BLOCK)
        s = lax.dot_general(
            queries, k_ref[0, pl.ds(start, KEY_BLOCK), :], dims, preferred_element_type=jnp.float32
        )
        pos = start + lax.broadcasted_iota(jnp.int32, (1, KEY_BLOCK), 1)
        s = jnp.where(pos < length, s * scale, neg_large)
        scores[b] = s
        top = maxes[...]
        for i in range(KEY_BLOCK // HD):
            top = jnp.maximum(top, s[:, i * HD : (i + 1) * HD])
        maxes[...] = top
        return carry

    lax.fori_loop(0, blocks, score, 0)
    row_max = jnp.maximum(
        jnp.max(maxes[...], axis=1, keepdims=True), jnp.max(tree, axis=1, keepdims=True)
    )
    tree_weights = jnp.exp(tree - row_max)
    total = jnp.sum(tree_weights, axis=1, keepdims=True)
    acc = jnp.dot(
        tree_weights.astype(jnp.bfloat16), tv_ref[...], preferred_element_type=jnp.float32
    )

    def absorb(b, carry):
        acc, sums = carry
        start = pl.multiple_of(b * KEY_BLOCK, KEY_BLOCK)
        w = jnp.exp(scores[b] - row_max)
        for i in range(KEY_BLOCK // HD):
            sums = sums + w[:, i * HD : (i + 1) * HD]
        acc = acc + jnp.dot(
            w.astype(jnp.bfloat16),
            v_ref[0, pl.ds(start, KEY_BLOCK), :],
            preferred_element_type=jnp.float32,
        )
        return acc, sums

    acc, sums = lax.fori_loop(0, blocks, absorb, (acc, jnp.zeros((rows, HD), jnp.float32)))
    total = total + jnp.sum(sums, axis=1, keepdims=True)
    attended = (acc / total).astype(out_ref.dtype)
    for g in range(GROUP):
        out_ref[:, g * HD : (g + 1) * HD] = attended[g * nodes : (g + 1) * nodes]


def attention(queries, tree_keys, tree_values, cache_keys, cache_values, cache_lens, parents):
    requests, nodes = parents.shape
    cache = cache_keys.shape[1]
    rows = nodes * GROUP
    per_node = lambda width: pl.BlockSpec((nodes, width), lambda r, lens: (r, 0))
    per_cache = pl.BlockSpec((1, cache, HD), lambda r, lens: (r, 0, 0))
    return pl.pallas_call(
        attention_kernel,
        grid_spec=pltpu.PrefetchScalarGridSpec(
            num_scalar_prefetch=1,
            grid=(requests,),
            in_specs=[
                pl.BlockSpec((1, nodes, 1), lambda r, lens: (r, 0, 0)),
                per_node(GROUP * HD),
                per_node(HD),
                per_node(HD),
                per_cache,
                per_cache,
            ],
            out_specs=per_node(GROUP * HD),
            scratch_shapes=[
                pltpu.VMEM((cache // KEY_BLOCK, rows, KEY_BLOCK), jnp.float32),
                pltpu.VMEM((rows, HD), jnp.float32),
            ],
        ),
        out_shape=jax.ShapeDtypeStruct(queries.shape, jnp.bfloat16),
        compiler_params=pltpu.CompilerParams(vmem_limit_bytes=62 * 1024 * 1024),
        cost_estimate=pl.CostEstimate(
            flops=requests * rows * cache * HD * 8,
            bytes_accessed=requests * cache * HD * 4,
            transcendentals=requests * rows * cache,
        ),
        name="attention",
    )(cache_lens, parents[:, :, None], queries, tree_keys, tree_values, cache_keys, cache_values)


def home_kernel(place_ref, residual_ref, *refs):
    pieces, out_ref = refs[:Y], refs[Y]
    width = pieces[0].shape[1]
    for q, piece in enumerate(pieces):
        columns = pl.ds(pl.multiple_of(place_ref[q] * width, width), width)
        out_ref[:, columns] = (
            residual_ref[:, columns].astype(jnp.float32) + piece[...].astype(jnp.float32)
        ).astype(out_ref.dtype)


def add_at_home(residual, pieces, places):
    return pl.pallas_call(
        home_kernel,
        in_specs=[pl.BlockSpec(memory_space=pltpu.SMEM)]
        + [pl.BlockSpec(memory_space=pltpu.VMEM)] * (1 + Y),
        out_specs=pl.BlockSpec(memory_space=pltpu.VMEM),
        out_shape=jax.ShapeDtypeStruct(residual.shape, residual.dtype),
        cost_estimate=pl.CostEstimate(
            flops=residual.size, bytes_accessed=residual.size * 6, transcendentals=0
        ),
        name="home",
    )(places, residual, *pieces)


def owner_kernel(want_ref, come_ref, *refs):
    blocks, outs = refs[:Z], refs[Z:]
    for r, out in enumerate(outs):
        for d, block in enumerate(blocks):

            @pl.when(want_ref[r] == d)
            def _():
                out[...] = (
                    block[...].astype(jnp.float32) + come_ref[d // 2].astype(jnp.float32)
                ).astype(out.dtype)


def owner_sums(blocks, come, want):
    shape = blocks[0].shape
    return pl.pallas_call(
        owner_kernel,
        in_specs=[pl.BlockSpec(memory_space=pltpu.SMEM)]
        + [pl.BlockSpec(memory_space=pltpu.VMEM)] * (1 + Z),
        out_specs=[pl.BlockSpec(memory_space=pltpu.VMEM)] * X,
        out_shape=[jax.ShapeDtypeStruct(shape, jnp.float32)]
        + [jax.ShapeDtypeStruct(shape, jnp.bfloat16)] * (X - 1),
        cost_estimate=pl.CostEstimate(
            flops=blocks[0].size * X, bytes_accessed=blocks[0].size * 24, transcendentals=0
        ),
        name="owner_sums",
    )(want, come, *blocks)


def place_kernel(at_ref, *refs):
    parts, out_ref = refs[:Y], refs[Y]
    for r in range(Z):
        for q, part in enumerate(parts):
            out_ref[(at_ref[0] + Z - r) % Z, (at_ref[1] + Y - q) % Y] = part[r]


def place_accepted(parts, at):
    _, count, width = parts[0].shape
    return pl.pallas_call(
        place_kernel,
        in_specs=[pl.BlockSpec(memory_space=pltpu.SMEM)]
        + [pl.BlockSpec(memory_space=pltpu.VMEM)] * Y,
        out_specs=pl.BlockSpec(memory_space=pltpu.VMEM),
        out_shape=jax.ShapeDtypeStruct((Z, Y, count, width), parts[0].dtype),
        cost_estimate=pl.CostEstimate(
            flops=parts[0].size, bytes_accessed=parts[0].size * 16, transcendentals=0
        ),
        name="place_accepted",
    )(at, *parts)


def device(z, y, j):
    return (z * Y + y) * X * C + j


def shift_z(value, by):
    pairs = [(z * Y + y, (z + by) % Z * Y + y) for z in range(Z) for y in range(Y)]
    return lax.ppermute(value, "dp", pairs)


def shift_y(value, by):
    pairs = [(z * Y + y, z * Y + (y + by) % Y) for z in range(Z) for y in range(Y)]
    return lax.ppermute(value, "dp", pairs)


def shift_x(value, by):
    pairs = [(x * C + c, (x + by) % X * C + c) for x in range(X) for c in range(C)]
    return lax.ppermute(value, "mp", pairs)


def swap_core(value):
    return lax.ppermute(value, "mp", [(j, j ^ 1) for j in range(X * C)])


def per_device(
    queries,
    tree_keys,
    tree_values,
    cache_keys,
    cache_values,
    cache_lens,
    parents,
    accepted_nodes,
    residual,
    out_weight,
):
    dp, mp = lax.axis_index("dp"), lax.axis_index("mp")
    z, y, x, c = dp // Y, dp % Y, mp // C, mp % C
    requests, nodes = parents.shape
    accepted = accepted_nodes.shape[1]
    rows = requests * nodes
    count = requests * accepted
    inner, width = out_weight.shape
    f32, bf16 = jnp.float32, jnp.bfloat16

    weights = [out_weight] + [None] * (Z - 1)
    ahead = behind = out_weight
    for d in range(1, Z // 2):
        ahead, behind = shift_z(ahead, -1), shift_z(behind, 1)
        weights[d], weights[Z - d] = ahead, behind
    half = inner // 2
    low, high = shift_z(ahead[:half], -1), shift_z(behind[half:], 1)
    across = [out_weight] + [shift_y(out_weight, q) for q in range(1, Y)]

    attended = attention(
        queries, tree_keys, tree_values, cache_keys, cache_values, cache_lens, parents
    )
    node_rows = (jnp.arange(requests, dtype=jnp.int32)[:, None] * nodes + accepted_nodes).reshape(-1)
    gathered = [attended] + [shift_y(attended, q) for q in range(1, Y)]

    picked = jnp.take(attended, node_rows, axis=0)
    picked = [picked] + [shift_z(picked, r) for r in range(1, Z)]
    picked = jnp.concatenate(picked, axis=0)
    picked_part = jnp.concatenate(
        [jnp.dot(picked, w, preferred_element_type=f32).astype(bf16) for w in across], axis=1
    )
    picked_sum = lax.all_to_all(picked_part.reshape(Z, count, Y * width), "mp", 0, 0, tiled=True)
    picked_sum = picked_sum.astype(f32).sum(axis=0).astype(bf16)
    pairs = [
        (device(zz, yy, j), device((zz - j) % Z, yy, zz))
        for zz in range(Z)
        for yy in range(Y)
        for j in range(X * C)
    ]
    picked_sum = lax.ppermute(picked_sum, ("dp", "mp"), pairs)
    tile = add_at_home(
        jnp.take(residual, node_rows, axis=0),
        [picked_sum[:, q * width : (q + 1) * width] for q in range(Y)],
        (y - jnp.arange(Y)) % Y,
    )
    tiles = jnp.stack([tile] + [shift_z(tile, r) for r in range(1, Z)])
    parts = [tiles] + [shift_y(tiles, q) for q in range(1, Y)]
    accepted_hidden = place_accepted(parts, jnp.stack([z, y])).reshape(Z * Y * count, Y * width)

    gathered = jnp.concatenate(gathered, axis=0)
    partial = [
        jnp.dot(gathered, w, preferred_element_type=f32).astype(bf16) if d != Z // 2 else None
        for d, w in enumerate(weights)
    ]
    partial[Z // 2] = (
        jnp.dot(gathered[:, :half], low, preferred_element_type=f32)
        + jnp.dot(gathered[:, half:], high, preferred_element_type=f32)
    ).astype(bf16)
    odd = (z + c) % 2
    come = swap_core(
        jnp.stack([jnp.where(odd == 0, partial[2 * e + 1], partial[2 * e]) for e in range(X)]),
    )
    want = (x + jnp.arange(X) - (z + odd) // 2) % X * 2 + odd
    own, *sent = owner_sums(partial, come, want)
    for by in range(1, X):
        own = own + shift_x(sent[by - 1], by).astype(f32)
    own = own.astype(bf16)
    home = [own[:rows]] + [shift_y(own[q * rows : (q + 1) * rows], -q) for q in range(1, Y)]
    tree_hidden = add_at_home(residual, home, (y + jnp.arange(Y)) % Y)
    return (tree_hidden, accepted_hidden)


def solution(mesh):
    placed = (
        P("dp", "mp"),
        P("dp", "mp"),
        P("dp", "mp"),
        P("dp", None, "mp"),
        P("dp", None, "mp"),
        P("dp"),
        P("dp", None),
        P("dp", None),
        P("dp", "mp"),
        P("mp", "dp"),
    )

    return jax.shard_map(
        per_device,
        mesh=mesh,
        in_specs=placed,
        out_specs=(P("dp", "mp"), P(None, "mp")),
        check_vma=False,
    )
```

profile of v0, /device:TPU:8, one launch (start us, length us, event | category | flops | bytes accessed | tf_op | source)
XLA Modules:
  0.0 194.4 jit_solution(4864370074554480611)
XLA Ops:
  4.5 16.7 %attention.1 = bf16[128,1024]{1,0:T(8,128)(2,1)} custom-call(s32[2]{0:T(128)} %lens_ref.1, s32[2,64,1]{2,1,0:T(8,128)} %copy.12.parents_ref, bf16[128,1024]{1,0:T(8,128)(2,1)} %q_ref.1, bf16[128,128]{1,0:T(8,128)(2,1)} %tk_ref.1, bf16[128,128]{1,0:T(8,128)(2,1)} %tv_ref.1, bf16[2,4096,128]{2,1,0:T(8,128)(2,1)} %k_ref.1, bf16[2,4096,128]{2,1,0:T(8,128)(2,1)} %v_ref.1), custom_call_target="tpu_custom_call" | custom-call | flops 4294967296 | bytes 4194304 | tf_op jit(solution)/shard_map/attention/pallas_call | solution.py:94
  26.5 2.4 %collective-permute-start.22 = (bf16[16,1024]{1,0:T(8,128)(2,1)S(1)}, bf16[16,1024]{1,0:T(8,128)(2,1)S(1)}, u32[]{:S(2)}, u32[]{:S(2)}) collective-permute-start(bf16[16,1024]{1,0:T(8,128)(2,1)S(1)} %get-tuple-element.12), channel_id=1, source_target_pairs={{0,160},{8,168},{16,176},{24,184},{32,192},{40,200},{48,208},{56,2... | collective-permute-start | bytes 98312 | tf_op jit(solution)/shard_map/ppermute | solution.py:204
  28.9 4.1 %collective-permute-start.21 = (bf16[16,1024]{1,0:T(8,128)(2,1)S(1)}, bf16[16,1024]{1,0:T(8,128)(2,1)S(1)}, u32[]{:S(2)}, u32[]{:S(2)}) collective-permute-start(bf16[16,1024]{1,0:T(8,128)(2,1)S(1)} %get-tuple-element.12), channel_id=1, source_target_pairs={{0,128},{8,136},{16,144},{24,152},{32,160},{40,168},{48,176},{56,1... | collective-permute-start | bytes 98312 | tf_op jit(solution)/shard_map/ppermute | solution.py:204
  34.8 3.3 %collective-permute-done.18 = bf16[16,1024]{1,0:T(8,128)(2,1)S(1)} collective-permute-done((bf16[16,1024]{1,0:T(8,128)(2,1)S(1)}, bf16[16,1024]{1,0:T(8,128)(2,1)S(1)}, u32[]{:S(2)}, u32[]{:S(2)}) %collective-permute-start.18) | collective-permute-done | bytes 32800 | tf_op jit(solution)/shard_map/ppermute | solution.py:204
  38.1 6.4 %collective-permute-done.19 = bf16[16,1024]{1,0:T(8,128)(2,1)S(1)} collective-permute-done((bf16[16,1024]{1,0:T(8,128)(2,1)S(1)}, bf16[16,1024]{1,0:T(8,128)(2,1)S(1)}, u32[]{:S(2)}, u32[]{:S(2)}) %collective-permute-start.19) | collective-permute-done | bytes 32800 | tf_op jit(solution)/shard_map/ppermute | solution.py:204
  44.5 6.9 %collective-permute-done.20 = bf16[16,1024]{1,0:T(8,128)(2,1)S(1)} collective-permute-done((bf16[16,1024]{1,0:T(8,128)(2,1)S(1)}, bf16[16,1024]{1,0:T(8,128)(2,1)S(1)}, u32[]{:S(2)}, u32[]{:S(2)}) %collective-permute-start.20) | collective-permute-done | bytes 32800 | tf_op jit(solution)/shard_map/ppermute | solution.py:204
  52.6 2.6 %collective-permute-start.1 = (bf16[128,1024]{1,0:T(8,128)(2,1)}, bf16[128,1024]{1,0:T(8,128)(2,1)S(1)}, u32[]{:S(2)}, u32[]{:S(2)}) collective-permute-start(bf16[128,1024]{1,0:T(8,128)(2,1)} %attention.1), channel_id=1, source_target_pairs={{0,16},{8,24},{16,0},{24,8},{32,48},{40,56},{48,32},{56,40},{64,80... | collective-permute-start | bytes 786440 | tf_op jit(solution)/shard_map/ppermute | solution.py:209
  57.0 3.6 %collective-permute-done.2 = bf16[128,1024]{1,0:T(8,128)(2,1)S(1)} collective-permute-done((bf16[128,1024]{1,0:T(8,128)(2,1)}, bf16[128,1024]{1,0:T(8,128)(2,1)S(1)}, u32[]{:S(2)}, u32[]{:S(2)}) %collective-permute-start.2) | collective-permute-done | bytes 262176 | tf_op jit(solution)/shard_map/ppermute | solution.py:209
  60.6 4.1 %collective-permute-done.1 = bf16[128,1024]{1,0:T(8,128)(2,1)S(1)} collective-permute-done((bf16[128,1024]{1,0:T(8,128)(2,1)}, bf16[128,1024]{1,0:T(8,128)(2,1)S(1)}, u32[]{:S(2)}, u32[]{:S(2)}) %collective-permute-start.1) | collective-permute-done | bytes 262176 | tf_op jit(solution)/shard_map/ppermute | solution.py:209
  64.9 3.9 %collective-permute-done = bf16[128,1024]{1,0:T(8,128)(2,1)S(1)} collective-permute-done((bf16[128,1024]{1,0:T(8,128)(2,1)}, bf16[128,1024]{1,0:T(8,128)(2,1)S(1)}, u32[]{:S(2)}, u32[]{:S(2)}) %collective-permute-start) | collective-permute-done | bytes 262176 | tf_op jit(solution)/shard_map/ppermute | solution.py:209
  71.4 8.6 %collective-permute-done.25 = bf16[1024,256]{1,0:T(8,128)(2,1)S(1)} collective-permute-done((bf16[1024,256]{1,0:T(8,128)(2,1)S(1)}, bf16[1024,256]{1,0:T(8,128)(2,1)S(1)}, u32[]{:S(2)}, u32[]{:S(2)}) %collective-permute-start.25) | collective-permute-done | bytes 524320 | tf_op jit(solution)/shard_map/ppermute | solution.py:209
  80.2 4.9 %collective-permute-done.27 = bf16[1024,256]{1,0:T(8,128)(2,1)S(1)} collective-permute-done((bf16[1024,256]{1,0:T(8,128)(2,1)S(1)}, bf16[1024,256]{1,0:T(8,128)(2,1)S(1)}, u32[]{:S(2)}, u32[]{:S(2)}) %collective-permute-start.27) | collective-permute-done | bytes 524320 | tf_op jit(solution)/shard_map/ppermute | solution.py:209
  86.4 4.3 %all-to-all-start = ((bf16[8,16,1024]{2,1,0:T(8,128)(2,1)}), bf16[8,16,1024]{2,1,0:T(8,128)(2,1)S(1)}, u32[]{:S(2)}, u32[]{:S(2)}) async-start(bf16[8,16,1024]{2,1,0:T(8,128)(2,1)} %bitcast.7), calls=%async_computation | async-start | bytes 524288 | tf_op jit(solution)/shard_map/all_to_all | solution.py:263
  92.3 3.3 %collective-permute-start.4 = (bf16[1024,256]{1,0:T(8,128)(2,1)}, bf16[1024,256]{1,0:T(8,128)(2,1)}, u32[]{:S(2)}, u32[]{:S(2)}) collective-permute-start(bf16[1024,256]{1,0:T(8,128)(2,1)} %collective-permute-done.3), channel_id=1, source_target_pairs={{0,224},{8,232},{16,240},{24,248},{32,0},{40,8},{48,16},{56,24},{6... | collective-permute-start | bytes 1572872 | tf_op jit(solution)/shard_map/ppermute | solution.py:204
  101.0 11.9 %collective-permute-start.35 = (bf16[16,1024]{1,0:T(8,128)(2,1)}, bf16[16,1024]{1,0:T(8,128)(2,1)S(1)}, u32[]{:S(2)}, u32[]{:S(2)}) collective-permute-start(bf16[16,1024]{1,0:T(8,128)(2,1)} %home.3), channel_id=1, source_target_pairs={{0,224},{8,232},{16,240},{24,248},{32,0},{40,8},{48,16},{56,24},{6... | collective-permute-start | bytes 98312 | tf_op jit(solution)/shard_map/ppermute | solution.py:204
  112.9 4.2 %collective-permute-start.34 = (bf16[16,1024]{1,0:T(8,128)(2,1)}, bf16[16,1024]{1,0:T(8,128)(2,1)S(1)}, u32[]{:S(2)}, u32[]{:S(2)}) collective-permute-start(bf16[16,1024]{1,0:T(8,128)(2,1)} %home.3), channel_id=1, source_target_pairs={{0,192},{8,200},{16,208},{24,216},{32,224},{40,232},{48,240},{56,2... | collective-permute-start | bytes 98312 | tf_op jit(solution)/shard_map/ppermute | solution.py:204
  124.4 8.2 %collective-permute-done.8 = bf16[1024,256]{1,0:T(8,128)(2,1)S(1)} collective-permute-done((bf16[1024,256]{1,0:T(8,128)(2,1)}, bf16[1024,256]{1,0:T(8,128)(2,1)S(1)}, u32[]{:S(2)}, u32[]{:S(2)}) %collective-permute-start.8) | collective-permute-done | bytes 524320 | tf_op jit(solution)/shard_map/ppermute | solution.py:204
  133.6 2.4 %collective-permute-start.9 = (bf16[512,256]{1,0:T(8,128)(2,1)S(1)}, bf16[512,256]{1,0:T(8,128)(2,1)S(1)}, u32[]{:S(2)}, u32[]{:S(2)}) collective-permute-start(bf16[512,256]{1,0:T(8,128)(2,1)S(1)} %slice.53), channel_id=1, source_target_pairs={{0,224},{8,232},{16,240},{24,248},{32,0},{40,8},{48,16},{56,24},{6... | collective-permute-start | bytes 786440 | tf_op jit(solution)/shard_map/ppermute | solution.py:204
  137.0 3.6 %collective-permute-done.10 = bf16[512,256]{1,0:T(8,128)(2,1)S(1)} collective-permute-done((bf16[512,256]{1,0:T(8,128)(2,1)S(1)}, bf16[512,256]{1,0:T(8,128)(2,1)S(1)}, u32[]{:S(2)}, u32[]{:S(2)}) %collective-permute-start.10) | collective-permute-done | bytes 262176 | tf_op jit(solution)/shard_map/ppermute | solution.py:204
  143.1 3.3 %collective-permute-done.29 = bf16[16,1024]{1,0:T(8,128)(2,1)S(1)} collective-permute-done((bf16[16,1024]{1,0:T(8,128)(2,1)S(1)}, bf16[16,1024]{1,0:T(8,128)(2,1)S(1)}, u32[]{:S(2)}, u32[]{:S(2)}) %collective-permute-start.29) | collective-permute-done | bytes 32800 | tf_op jit(solution)/shard_map/ppermute | solution.py:204
  148.3 5.4 %collective-permute-done.31 = bf16[16,1024]{1,0:T(8,128)(2,1)S(1)} collective-permute-done((bf16[16,1024]{1,0:T(8,128)(2,1)S(1)}, bf16[16,1024]{1,0:T(8,128)(2,1)S(1)}, u32[]{:S(2)}, u32[]{:S(2)}) %collective-permute-start.31) | collective-permute-done | bytes 32800 | tf_op jit(solution)/shard_map/ppermute | solution.py:204
  153.8 3.3 %collective-permute-start.32 = (bf16[16,1024]{1,0:T(8,128)(2,1)S(1)}, bf16[16,1024]{1,0:T(8,128)(2,1)S(1)}, u32[]{:S(2)}, u32[]{:S(2)}) collective-permute-start(bf16[16,1024]{1,0:T(8,128)(2,1)S(1)} %copy-done.17), channel_id=1, source_target_pairs={{0,128},{8,136},{16,144},{24,152},{32,160},{40,168},{48,176},{56,1... | collective-permute-start | bytes 98312 | tf_op jit(solution)/shard_map/ppermute | solution.py:204
  157.1 4.5 %collective-permute-done.32 = bf16[16,1024]{1,0:T(8,128)(2,1)S(1)} collective-permute-done((bf16[16,1024]{1,0:T(8,128)(2,1)S(1)}, bf16[16,1024]{1,0:T(8,128)(2,1)S(1)}, u32[]{:S(2)}, u32[]{:S(2)}) %collective-permute-start.32) | collective-permute-done | bytes 32800 | tf_op jit(solution)/shard_map/ppermute | solution.py:204
  162.6 3.4 %owner_sums.1 = (f32[512,256]{1,0:T(8,128)}, bf16[512,256]{1,0:T(8,128)(2,1)}, bf16[512,256]{1,0:T(8,128)(2,1)}, bf16[512,256]{1,0:T(8,128)(2,1)}) custom-call(s32[4]{0:T(128)} %fusion.5.want_ref, bf16[4,512,256]{2,1,0:T(8,128)(2,1)} %copy-done.1, bf16[512,256]{1,0:T(8,128)(2,1)} %copy-done.3, bf16[512,256]{1,0:T(8,128)(2,1)} %copy-done.5, ...), custom_call_target="tpu_custom_call" | custom-call | flops 524288 | bytes 3145728 | tf_op jit(solution)/shard_map/owner_sums/pallas_call | solution.py:162
  166.0 3.5 %collective-permute-start.13 = (bf16[512,256]{1,0:T(8,128)(2,1)}, bf16[512,256]{1,0:T(8,128)(2,1)S(1)}, u32[]{:S(2)}, u32[]{:S(2)}) collective-permute-start(bf16[512,256]{1,0:T(8,128)(2,1)} %get-tuple-element.9), channel_id=1, source_target_pairs={{0,4},{1,5},{2,6},{3,7},{4,0},{5,1},{6,2},{7,3},{8,12},{9,13},{10,... | collective-permute-start | bytes 786440 | tf_op jit(solution)/shard_map/ppermute | solution.py:214
  169.8 3.8 %collective-permute-start.38 = (bf16[8,16,1024]{2,1,0:T(8,128)(2,1)S(1)}, bf16[8,16,1024]{2,1,0:T(8,128)(2,1)S(1)}, u32[]{:S(2)}, u32[]{:S(2)}) collective-permute-start(bf16[8,16,1024]{2,1,0:T(8,128)(2,1)S(1)} %constant_dynamic-update-slice_fusion.8.refs_0_), channel_id=1, source_target_pairs={{0,24},{8,0},{16,8},{24,16},{32,56},{40,32},{48,40},{56,48},{64,88... | collective-permute-start | bytes 786440 | tf_op jit(solution)/shard_map/ppermute | solution.py:209
  173.7 2.5 %collective-permute-done.12 = bf16[512,256]{1,0:T(8,128)(2,1)S(1)} collective-permute-done((bf16[512,256]{1,0:T(8,128)(2,1)}, bf16[512,256]{1,0:T(8,128)(2,1)S(1)}, u32[]{:S(2)}, u32[]{:S(2)}) %collective-permute-start.12) | collective-permute-done | bytes 262176 | tf_op jit(solution)/shard_map/ppermute | solution.py:214
  177.3 2.9 %collective-permute-done.13 = bf16[512,256]{1,0:T(8,128)(2,1)S(1)} collective-permute-done((bf16[512,256]{1,0:T(8,128)(2,1)}, bf16[512,256]{1,0:T(8,128)(2,1)S(1)}, u32[]{:S(2)}, u32[]{:S(2)}) %collective-permute-start.13) | collective-permute-done | bytes 262176 | tf_op jit(solution)/shard_map/ppermute | solution.py:214
  182.3 2.0 %collective-permute-start.17 = (bf16[128,256]{1,0:T(8,128)(2,1)S(1)}, bf16[128,256]{1,0:T(8,128)(2,1)S(1)}, u32[]{:S(2)}, u32[]{:S(2)}) collective-permute-start(bf16[128,256]{1,0:T(8,128)(2,1)S(1)} %get-tuple-element.13), channel_id=1, source_target_pairs={{0,8},{8,16},{16,24},{24,0},{32,40},{40,48},{48,56},{56,32},{64,72... | collective-permute-start | bytes 196616 | tf_op jit(solution)/shard_map/ppermute | solution.py:209
  184.3 3.2 %collective-permute-start.16 = (bf16[128,256]{1,0:T(8,128)(2,1)S(1)}, bf16[128,256]{1,0:T(8,128)(2,1)S(1)}, u32[]{:S(2)}, u32[]{:S(2)}) collective-permute-start(bf16[128,256]{1,0:T(8,128)(2,1)S(1)} %get-tuple-element.14), channel_id=1, source_target_pairs={{0,16},{8,24},{16,0},{24,8},{32,48},{40,56},{48,32},{56,40},{64,80... | collective-permute-start | bytes 196616 | tf_op jit(solution)/shard_map/ppermute | solution.py:209
  189.6 2.3 %place_accepted.1 = bf16[8,4,16,1024]{3,2,1,0:T(8,128)(2,1)} custom-call(s32[2]{0:T(128)} %pad_add_fusion.at_ref, bf16[8,16,1024]{2,1,0:T(8,128)(2,1)} %copy-done.11, bf16[8,16,1024]{2,1,0:T(8,128)(2,1)} %copy-done.14, bf16[8,16,1024]{2,1,0:T(8,128)(2,1)} %copy-done.13, bf16[8,16,1024]{2,1,0:T(8,128)(2,1)} %copy-done.12), custom_call_target="tpu_custom_call" | custom-call | flops 131072 | bytes 2097152 | tf_op jit(solution)/shard_map/place_accepted/pallas_call | solution.py:185
  192.6 1.8 home.2
  (150 shorter events, 45.7 us)
Async XLA Ops:
  23.6 33.2 %collective-permute-start.24 = (bf16[16,1024]{1,0:T(8,128)(2,1)S(1)}, bf16[16,1024]{1,0:T(8,128)(2,1)S(1)}, u32[]{:S(2)}, u32[]{:S(2)}) collective-permute-start(bf16[16,1024]{1,0:T(8,128)(2,1)S(1)} %get-tuple-element.12), channel_id=1, source_target_pairs={{0,224},{8,232},{16,240},{24,248},{32,0},{40,8},{48,16},{56,24},{6... | collective-permute-start | bytes 98312 | tf_op jit(solution)/shard_map/ppermute | solution.py:204
  24.7 30.7 %collective-permute-start.23 = (bf16[16,1024]{1,0:T(8,128)(2,1)S(1)}, bf16[16,1024]{1,0:T(8,128)(2,1)S(1)}, u32[]{:S(2)}, u32[]{:S(2)}) collective-permute-start(bf16[16,1024]{1,0:T(8,128)(2,1)S(1)} %get-tuple-element.12), channel_id=1, source_target_pairs={{0,192},{8,200},{16,208},{24,216},{32,224},{40,232},{48,240},{56,2... | collective-permute-start | bytes 98312 | tf_op jit(solution)/shard_map/ppermute | solution.py:204
  26.5 28.6 %collective-permute-start.22 = (bf16[16,1024]{1,0:T(8,128)(2,1)S(1)}, bf16[16,1024]{1,0:T(8,128)(2,1)S(1)}, u32[]{:S(2)}, u32[]{:S(2)}) collective-permute-start(bf16[16,1024]{1,0:T(8,128)(2,1)S(1)} %get-tuple-element.12), channel_id=1, source_target_pairs={{0,160},{8,168},{16,176},{24,184},{32,192},{40,200},{48,208},{56,2... | collective-permute-start | bytes 98312 | tf_op jit(solution)/shard_map/ppermute | solution.py:204
  28.9 23.6 %collective-permute-start.21 = (bf16[16,1024]{1,0:T(8,128)(2,1)S(1)}, bf16[16,1024]{1,0:T(8,128)(2,1)S(1)}, u32[]{:S(2)}, u32[]{:S(2)}) collective-permute-start(bf16[16,1024]{1,0:T(8,128)(2,1)S(1)} %get-tuple-element.12), channel_id=1, source_target_pairs={{0,128},{8,136},{16,144},{24,152},{32,160},{40,168},{48,176},{56,1... | collective-permute-start | bytes 98312 | tf_op jit(solution)/shard_map/ppermute | solution.py:204
  51.4 9.2 %collective-permute-start.2 = (bf16[128,1024]{1,0:T(8,128)(2,1)}, bf16[128,1024]{1,0:T(8,128)(2,1)S(1)}, u32[]{:S(2)}, u32[]{:S(2)}) collective-permute-start(bf16[128,1024]{1,0:T(8,128)(2,1)} %attention.1), channel_id=1, source_target_pairs={{0,24},{8,0},{16,8},{24,16},{32,56},{40,32},{48,40},{56,48},{64,88... | collective-permute-start | bytes 786440 | tf_op jit(solution)/shard_map/ppermute | solution.py:209
  52.6 12.2 %collective-permute-start.1 = (bf16[128,1024]{1,0:T(8,128)(2,1)}, bf16[128,1024]{1,0:T(8,128)(2,1)S(1)}, u32[]{:S(2)}, u32[]{:S(2)}) collective-permute-start(bf16[128,1024]{1,0:T(8,128)(2,1)} %attention.1), channel_id=1, source_target_pairs={{0,16},{8,24},{16,0},{24,8},{32,48},{40,56},{48,32},{56,40},{64,80... | collective-permute-start | bytes 786440 | tf_op jit(solution)/shard_map/ppermute | solution.py:209
  55.2 13.7 %collective-permute-start = (bf16[128,1024]{1,0:T(8,128)(2,1)}, bf16[128,1024]{1,0:T(8,128)(2,1)S(1)}, u32[]{:S(2)}, u32[]{:S(2)}) collective-permute-start(bf16[128,1024]{1,0:T(8,128)(2,1)} %attention.1), channel_id=1, source_target_pairs={{0,8},{8,16},{16,24},{24,0},{32,40},{40,48},{48,56},{56,32},{64,72... | collective-permute-start | bytes 786440 | tf_op jit(solution)/shard_map/ppermute | solution.py:209
  55.5 24.5 %collective-permute-start.25 = (bf16[1024,256]{1,0:T(8,128)(2,1)S(1)}, bf16[1024,256]{1,0:T(8,128)(2,1)S(1)}, u32[]{:S(2)}, u32[]{:S(2)}) collective-permute-start(bf16[1024,256]{1,0:T(8,128)(2,1)S(1)} %copy-done.10), channel_id=1, source_target_pairs={{0,8},{8,16},{16,24},{24,0},{32,40},{40,48},{48,56},{56,32},{64,72... | collective-permute-start | bytes 1572872 | tf_op jit(solution)/shard_map/ppermute | solution.py:209
  56.8 33.9 %collective-permute-start.6 = (bf16[1024,256]{1,0:T(8,128)(2,1)S(1)}, bf16[1024,256]{1,0:T(8,128)(2,1)}, u32[]{:S(2)}, u32[]{:S(2)}) collective-permute-start(bf16[1024,256]{1,0:T(8,128)(2,1)S(1)} %copy-done.10), channel_id=1, source_target_pairs={{0,32},{8,40},{16,48},{24,56},{32,64},{40,72},{48,80},{56,88},{64,... | collective-permute-start | bytes 1572872 | tf_op jit(solution)/shard_map/ppermute | solution.py:204
  60.6 31.7 %collective-permute-start.3 = (bf16[1024,256]{1,0:T(8,128)(2,1)S(1)}, bf16[1024,256]{1,0:T(8,128)(2,1)}, u32[]{:S(2)}, u32[]{:S(2)}) collective-permute-start(bf16[1024,256]{1,0:T(8,128)(2,1)S(1)} %copy-done.10), channel_id=1, source_target_pairs={{0,224},{8,232},{16,240},{24,248},{32,0},{40,8},{48,16},{56,24},{6... | collective-permute-start | bytes 1572872 | tf_op jit(solution)/shard_map/ppermute | solution.py:204
  64.8 20.4 %collective-permute-start.27 = (bf16[1024,256]{1,0:T(8,128)(2,1)S(1)}, bf16[1024,256]{1,0:T(8,128)(2,1)S(1)}, u32[]{:S(2)}, u32[]{:S(2)}) collective-permute-start(bf16[1024,256]{1,0:T(8,128)(2,1)S(1)} %copy-done.10), channel_id=1, source_target_pairs={{0,24},{8,0},{16,8},{24,16},{32,56},{40,32},{48,40},{56,48},{64,88... | collective-permute-start | bytes 1572872 | tf_op jit(solution)/shard_map/ppermute | solution.py:209
  68.8 16.6 %collective-permute-start.26 = (bf16[1024,256]{1,0:T(8,128)(2,1)S(1)}, bf16[1024,256]{1,0:T(8,128)(2,1)S(1)}, u32[]{:S(2)}, u32[]{:S(2)}) collective-permute-start(bf16[1024,256]{1,0:T(8,128)(2,1)S(1)} %copy-done.10), channel_id=1, source_target_pairs={{0,16},{8,24},{16,0},{24,8},{32,48},{40,56},{48,32},{56,40},{64,80... | collective-permute-start | bytes 1572872 | tf_op jit(solution)/shard_map/ppermute | solution.py:209
  86.4 11.8 %all-to-all-start = ((bf16[8,16,1024]{2,1,0:T(8,128)(2,1)}), bf16[8,16,1024]{2,1,0:T(8,128)(2,1)S(1)}, u32[]{:S(2)}, u32[]{:S(2)}) async-start(bf16[8,16,1024]{2,1,0:T(8,128)(2,1)} %bitcast.7), calls=%async_computation | async-start | bytes 524288 | tf_op jit(solution)/shard_map/all_to_all | solution.py:263
  90.7 27.2 %collective-permute-start.7 = (bf16[1024,256]{1,0:T(8,128)(2,1)}, bf16[1024,256]{1,0:T(8,128)(2,1)}, u32[]{:S(2)}, u32[]{:S(2)}) collective-permute-start(bf16[1024,256]{1,0:T(8,128)(2,1)} %collective-permute-done.6), channel_id=1, source_target_pairs={{0,32},{8,40},{16,48},{24,56},{32,64},{40,72},{48,80},{56,88},{64,... | collective-permute-start | bytes 1572872 | tf_op jit(solution)/shard_map/ppermute | solution.py:204
  92.3 27.3 %collective-permute-start.4 = (bf16[1024,256]{1,0:T(8,128)(2,1)}, bf16[1024,256]{1,0:T(8,128)(2,1)}, u32[]{:S(2)}, u32[]{:S(2)}) collective-permute-start(bf16[1024,256]{1,0:T(8,128)(2,1)} %collective-permute-done.3), channel_id=1, source_target_pairs={{0,224},{8,232},{16,240},{24,248},{32,0},{40,8},{48,16},{56,24},{6... | collective-permute-start | bytes 1572872 | tf_op jit(solution)/shard_map/ppermute | solution.py:204
  101.0 68.8 %collective-permute-start.35 = (bf16[16,1024]{1,0:T(8,128)(2,1)}, bf16[16,1024]{1,0:T(8,128)(2,1)S(1)}, u32[]{:S(2)}, u32[]{:S(2)}) collective-permute-start(bf16[16,1024]{1,0:T(8,128)(2,1)} %home.3), channel_id=1, source_target_pairs={{0,224},{8,232},{16,240},{24,248},{32,0},{40,8},{48,16},{56,24},{6... | collective-permute-start | bytes 98312 | tf_op jit(solution)/shard_map/ppermute | solution.py:204
  112.9 56.9 %collective-permute-start.34 = (bf16[16,1024]{1,0:T(8,128)(2,1)}, bf16[16,1024]{1,0:T(8,128)(2,1)S(1)}, u32[]{:S(2)}, u32[]{:S(2)}) collective-permute-start(bf16[16,1024]{1,0:T(8,128)(2,1)} %home.3), channel_id=1, source_target_pairs={{0,192},{8,200},{16,208},{24,216},{32,224},{40,232},{48,240},{56,2... | collective-permute-start | bytes 98312 | tf_op jit(solution)/shard_map/ppermute | solution.py:204
  117.1 44.5 %collective-permute-start.33 = (bf16[16,1024]{1,0:T(8,128)(2,1)}, bf16[16,1024]{1,0:T(8,128)(2,1)S(1)}, u32[]{:S(2)}, u32[]{:S(2)}) collective-permute-start(bf16[16,1024]{1,0:T(8,128)(2,1)} %home.3), channel_id=1, source_target_pairs={{0,160},{8,168},{16,176},{24,184},{32,192},{40,200},{48,208},{56,2... | collective-permute-start | bytes 98312 | tf_op jit(solution)/shard_map/ppermute | solution.py:204
  117.9 14.6 %collective-permute-start.8 = (bf16[1024,256]{1,0:T(8,128)(2,1)}, bf16[1024,256]{1,0:T(8,128)(2,1)S(1)}, u32[]{:S(2)}, u32[]{:S(2)}) collective-permute-start(bf16[1024,256]{1,0:T(8,128)(2,1)} %collective-permute-done.7), channel_id=1, source_target_pairs={{0,32},{8,40},{16,48},{24,56},{32,64},{40,72},{48,80},{56,88},{64,... | collective-permute-start | bytes 1572872 | tf_op jit(solution)/shard_map/ppermute | solution.py:204
  119.7 13.9 %collective-permute-start.5 = (bf16[1024,256]{1,0:T(8,128)(2,1)}, bf16[1024,256]{1,0:T(8,128)(2,1)S(1)}, u32[]{:S(2)}, u32[]{:S(2)}) collective-permute-start(bf16[1024,256]{1,0:T(8,128)(2,1)} %collective-permute-done.4), channel_id=1, source_target_pairs={{0,224},{8,232},{16,240},{24,248},{32,0},{40,8},{48,16},{56,24},{6... | collective-permute-start | bytes 1572872 | tf_op jit(solution)/shard_map/ppermute | solution.py:204
  132.6 8.0 %collective-permute-start.10 = (bf16[512,256]{1,0:T(8,128)(2,1)S(1)}, bf16[512,256]{1,0:T(8,128)(2,1)S(1)}, u32[]{:S(2)}, u32[]{:S(2)}) collective-permute-start(bf16[512,256]{1,0:T(8,128)(2,1)S(1)} %slice.55), channel_id=1, source_target_pairs={{0,32},{8,40},{16,48},{24,56},{32,64},{40,72},{48,80},{56,88},{64,... | collective-permute-start | bytes 786440 | tf_op jit(solution)/shard_map/ppermute | solution.py:204
  133.6 7.3 %collective-permute-start.9 = (bf16[512,256]{1,0:T(8,128)(2,1)S(1)}, bf16[512,256]{1,0:T(8,128)(2,1)S(1)}, u32[]{:S(2)}, u32[]{:S(2)}) collective-permute-start(bf16[512,256]{1,0:T(8,128)(2,1)S(1)} %slice.53), channel_id=1, source_target_pairs={{0,224},{8,232},{16,240},{24,248},{32,0},{40,8},{48,16},{56,24},{6... | collective-permute-start | bytes 786440 | tf_op jit(solution)/shard_map/ppermute | solution.py:204
  146.4 15.2 %collective-permute-start.11 = (bf16[4,512,256]{2,1,0:T(8,128)(2,1)S(1)}, bf16[4,512,256]{2,1,0:T(8,128)(2,1)S(1)}, u32[]{:S(2)}, u32[]{:S(2)}) collective-permute-start(bf16[4,512,256]{2,1,0:T(8,128)(2,1)S(1)} %pad_maximum_fusion.1), channel_id=1, source_target_pairs={{0,1},{1,0},{2,3},{3,2},{4,5},{5,4},{6,7},{7,6},{8,9},{9,8},{10,11... | collective-permute-start | bytes 3145736 | tf_op jit(solution)/shard_map/ppermute | solution.py:218
  153.8 7.8 %collective-permute-start.32 = (bf16[16,1024]{1,0:T(8,128)(2,1)S(1)}, bf16[16,1024]{1,0:T(8,128)(2,1)S(1)}, u32[]{:S(2)}, u32[]{:S(2)}) collective-permute-start(bf16[16,1024]{1,0:T(8,128)(2,1)S(1)} %copy-done.17), channel_id=1, source_target_pairs={{0,128},{8,136},{16,144},{24,152},{32,160},{40,168},{48,176},{56,1... | collective-permute-start | bytes 98312 | tf_op jit(solution)/shard_map/ppermute | solution.py:204
  166.0 10.2 %collective-permute-start.12 = (bf16[512,256]{1,0:T(8,128)(2,1)}, bf16[512,256]{1,0:T(8,128)(2,1)S(1)}, u32[]{:S(2)}, u32[]{:S(2)}) collective-permute-start(bf16[512,256]{1,0:T(8,128)(2,1)} %get-tuple-element.8), channel_id=1, source_target_pairs={{0,2},{1,3},{2,4},{3,5},{4,6},{5,7},{6,0},{7,1},{8,10},{9,11},{10,... | collective-permute-start | bytes 786440 | tf_op jit(solution)/shard_map/ppermute | solution.py:214
  166.0 14.2 %collective-permute-start.13 = (bf16[512,256]{1,0:T(8,128)(2,1)}, bf16[512,256]{1,0:T(8,128)(2,1)S(1)}, u32[]{:S(2)}, u32[]{:S(2)}) collective-permute-start(bf16[512,256]{1,0:T(8,128)(2,1)} %get-tuple-element.9), channel_id=1, source_target_pairs={{0,4},{1,5},{2,6},{3,7},{4,0},{5,1},{6,2},{7,3},{8,12},{9,13},{10,... | collective-permute-start | bytes 786440 | tf_op jit(solution)/shard_map/ppermute | solution.py:214
  169.5 11.0 %collective-permute-start.14 = (bf16[512,256]{1,0:T(8,128)(2,1)}, bf16[512,256]{1,0:T(8,128)(2,1)S(1)}, u32[]{:S(2)}, u32[]{:S(2)}) collective-permute-start(bf16[512,256]{1,0:T(8,128)(2,1)} %get-tuple-element.10), channel_id=1, source_target_pairs={{0,6},{1,7},{2,0},{3,1},{4,2},{5,3},{6,4},{7,5},{8,14},{9,15},{10,... | collective-permute-start | bytes 786440 | tf_op jit(solution)/shard_map/ppermute | solution.py:214
  169.8 17.7 %collective-permute-start.38 = (bf16[8,16,1024]{2,1,0:T(8,128)(2,1)S(1)}, bf16[8,16,1024]{2,1,0:T(8,128)(2,1)S(1)}, u32[]{:S(2)}, u32[]{:S(2)}) collective-permute-start(bf16[8,16,1024]{2,1,0:T(8,128)(2,1)S(1)} %constant_dynamic-update-slice_fusion.8.refs_0_), channel_id=1, source_target_pairs={{0,24},{8,0},{16,8},{24,16},{32,56},{40,32},{48,40},{56,48},{64,88... | collective-permute-start | bytes 786440 | tf_op jit(solution)/shard_map/ppermute | solution.py:209
  173.7 14.5 %collective-permute-start.37 = (bf16[8,16,1024]{2,1,0:T(8,128)(2,1)S(1)}, bf16[8,16,1024]{2,1,0:T(8,128)(2,1)S(1)}, u32[]{:S(2)}, u32[]{:S(2)}) collective-permute-start(bf16[8,16,1024]{2,1,0:T(8,128)(2,1)S(1)} %constant_dynamic-update-slice_fusion.8.refs_0_), channel_id=1, source_target_pairs={{0,16},{8,24},{16,0},{24,8},{32,48},{40,56},{48,32},{56,40},{64,80... | collective-permute-start | bytes 786440 | tf_op jit(solution)/shard_map/ppermute | solution.py:209
  176.2 12.0 %collective-permute-start.36 = (bf16[8,16,1024]{2,1,0:T(8,128)(2,1)S(1)}, bf16[8,16,1024]{2,1,0:T(8,128)(2,1)S(1)}, u32[]{:S(2)}, u32[]{:S(2)}) collective-permute-start(bf16[8,16,1024]{2,1,0:T(8,128)(2,1)S(1)} %constant_dynamic-update-slice_fusion.8.refs_0_), channel_id=1, source_target_pairs={{0,8},{8,16},{16,24},{24,0},{32,40},{40,48},{48,56},{56,32},{64,72... | collective-permute-start | bytes 786440 | tf_op jit(solution)/shard_map/ppermute | solution.py:209
  182.3 9.6 %collective-permute-start.17 = (bf16[128,256]{1,0:T(8,128)(2,1)S(1)}, bf16[128,256]{1,0:T(8,128)(2,1)S(1)}, u32[]{:S(2)}, u32[]{:S(2)}) collective-permute-start(bf16[128,256]{1,0:T(8,128)(2,1)S(1)} %get-tuple-element.13), channel_id=1, source_target_pairs={{0,8},{8,16},{16,24},{24,0},{32,40},{40,48},{48,56},{56,32},{64,72... | collective-permute-start | bytes 196616 | tf_op jit(solution)/shard_map/ppermute | solution.py:209
  184.3 7.6 %collective-permute-start.16 = (bf16[128,256]{1,0:T(8,128)(2,1)S(1)}, bf16[128,256]{1,0:T(8,128)(2,1)S(1)}, u32[]{:S(2)}, u32[]{:S(2)}) collective-permute-start(bf16[128,256]{1,0:T(8,128)(2,1)S(1)} %get-tuple-element.14), channel_id=1, source_target_pairs={{0,16},{8,24},{16,0},{24,8},{32,48},{40,56},{48,32},{56,40},{64,80... | collective-permute-start | bytes 196616 | tf_op jit(solution)/shard_map/ppermute | solution.py:209
  (29 other events, 290.7 us)
where the time goes:
time: 196 us; the launch traced here: 194 us
  waiting for transfers between devices  74.6 us (38%)
  starting transfers between devices  67 us (34%)
  Pallas kernels  25.7 us (13%)
  local copies, waits for them, and re-layouts  9.93 us (5%)
  matrix products  9.93 us (5%)
  other arithmetic  6.13 us (3%)
    ppermute x22, waiting for transfers between devices, shift_z(): return lax.ppermute(value, 'dp', pairs)  42.7 us
    ppermute x22, starting transfers between devices, shift_z(): return lax.ppermute(value, 'dp', pairs)  41.5 us
    ppermute x12, waiting for transfers between devices, shift_y(): return lax.ppermute(value, 'dp', pairs)  25.2 us
    pallas_call x1, Pallas kernels, attention(): pl.pallas_call(attention_kernel, grid_spec=pltpu.PrefetchScalarGridSpec(n...  16.7 us
    ppermute x12, starting transfers between devices, shift_y(): return lax.ppermute(value, 'dp', pairs)  16.7 us
    dot_general x7, matrix products, per_device(): jnp.dot(gathered, w, preferred_element_type=f32).astype(bf16)  8.4 us
    ppermute x3, waiting for transfers between devices, shift_x(): return lax.ppermute(value, 'mp', pairs)  5.74 us
    all_to_all x1, starting transfers between devices, per_device(): lax.all_to_all(picked_part.reshape(Z, count, Y * width), 'mp', 0, 0, tile...  4.32 us
  transfers between devices with their start and end apart: 40, of which 19 were waited for; matrix products, arithmetic and copies ran while one was open for 9% of the time, Pallas kernels for 4%

commit v1 on v0

v1 whole, which is shorter than its diff:
```python
import functools
import math

import jax
import jax.numpy as jnp
from jax import lax
from jax.experimental import pallas as pl
from jax.experimental.pallas import tpu as pltpu
from jax.sharding import PartitionSpec as P

HEADS = 64
KV_HEADS = 8
HD = 128
GROUP = HEADS // KV_HEADS
NODES, ACC = 64, 8
Z, Y, X, C = 8, 4, 4, 2
KEY_BLOCK = 1024
neg_large = -1e30


def attention_kernel(
    lens_ref,
    parents_ref,
    q_ref,
    tk_ref,
    tv_ref,
    k_ref,
    v_ref,
    accepted_ref,
    *rest,
    request,
):
    out_ref, picked_ref, scores, acc = rest[-4:]
    nodes = q_ref.shape[0]
    rows = nodes * GROUP
    f32, bf16 = jnp.float32, jnp.bfloat16
    factor = math.log2(math.e) / math.sqrt(HD)
    length = lens_ref[request]

    row = lax.broadcasted_iota(jnp.int32, (nodes, nodes), 0)
    col = lax.broadcasted_iota(jnp.int32, (nodes, nodes), 1)
    parents = parents_ref[request : request + 1, :]
    reached = ((parents == row) | (row == col)).astype(f32).astype(bf16)
    for _ in range((nodes - 1).bit_length()):
        squared = jnp.dot(reached, reached, preferred_element_type=f32)
        reached = jnp.minimum(squared, 1.0).astype(bf16)
    head = lax.broadcasted_iota(jnp.int32, (nodes, rows), 1) % nodes
    repeat = head == lax.broadcasted_iota(jnp.int32, (nodes, rows), 0)
    ancestor = jnp.dot(reached, repeat.astype(f32).astype(bf16), preferred_element_type=f32) > 0.5

    queries = jnp.concatenate([q_ref[:, g * HD : (g + 1) * HD] for g in range(GROUP)], axis=0)
    last, first = (((1,), (1,)), ((), ())), (((0,), (0,)), ((), ()))
    tree = lax.dot_general(tk_ref[...], queries, last, preferred_element_type=f32) * factor
    tree = jnp.where(ancestor, tree, neg_large)
    blocks = (length + KEY_BLOCK - 1) // KEY_BLOCK

    def score(b, top):
        start = pl.multiple_of(b * KEY_BLOCK, KEY_BLOCK)
        keys = k_ref[0, pl.ds(start, KEY_BLOCK), :]
        s = lax.dot_general(keys, queries, last, preferred_element_type=f32) * factor
        position = start + lax.broadcasted_iota(jnp.int32, (KEY_BLOCK, 1), 0)
        s = jnp.where(position < length, s, neg_large)
        scores[b] = s
        return jnp.maximum(top, jnp.max(s, axis=0, keepdims=True))

    top = lax.fori_loop(0, blocks, score, jnp.max(tree, axis=0, keepdims=True))
    weights = jnp.exp2(tree - top)
    total = jnp.sum(weights, axis=0, keepdims=True)
    acc[...] = lax.dot_general(
        tv_ref[...], weights.astype(bf16), first, preferred_element_type=f32
    )

    def absorb(b, total):
        start = pl.multiple_of(b * KEY_BLOCK, KEY_BLOCK)
        w = jnp.exp2(scores[b] - top)
        acc[...] += lax.dot_general(
            v_ref[0, pl.ds(start, KEY_BLOCK), :],
            w.astype(bf16),
            first,
            preferred_element_type=f32,
        )
        return total + jnp.sum(w, axis=0, keepdims=True)

    total = lax.fori_loop(0, blocks, absorb, total)
    attended = (acc[...] / total).T.astype(out_ref.dtype)
    accepted = accepted_ref[request : request + 1, :]
    hot = lax.broadcasted_iota(jnp.int32, (nodes, accepted.shape[1]), 0) == accepted
    hot = hot.astype(f32).astype(bf16)
    for g in range(GROUP):
        one = attended[g * nodes : (g + 1) * nodes]
        out_ref[:, g * HD : (g + 1) * HD] = one
        picked_ref[:, g * HD : (g + 1) * HD] = lax.dot_general(
            hot, one, first, preferred_element_type=f32
        ).astype(picked_ref.dtype)


def attention(request, earlier, inputs):
    _, parents, queries, _, _, cache_keys, _, accepted_nodes = inputs
    nodes = parents.shape[1]
    cache = cache_keys.shape[1]
    rows = nodes * GROUP
    count = accepted_nodes.shape[1]
    width = queries.shape[1]
    per_node = lambda size: pl.BlockSpec((nodes, size), lambda i, lens: (request, 0))
    per_cache = pl.BlockSpec((1, cache, HD), lambda i, lens: (request, 0, 0))
    whole = lambda array: pl.BlockSpec(array.shape, lambda i, lens: (0, 0))
    return pl.pallas_call(
        functools.partial(attention_kernel, request=request),
        grid_spec=pltpu.PrefetchScalarGridSpec(
            num_scalar_prefetch=1,
            grid=(1,),
            in_specs=[
                whole(parents),
                per_node(width),
                per_node(HD),
                per_node(HD),
                per_cache,
                per_cache,
                whole(accepted_nodes),
            ]
            + [pl.BlockSpec(memory_space=pl.ANY)] * len(earlier),
            out_specs=[
                per_node(width),
                pl.BlockSpec((count, width), lambda i, lens: (0, 0)),
            ],
            scratch_shapes=[
                pltpu.VMEM((cache // KEY_BLOCK, KEY_BLOCK, rows), jnp.float32),
                pltpu.VMEM((HD, rows), jnp.float32),
            ],
        ),
        out_shape=[
            jax.ShapeDtypeStruct(queries.shape, jnp.bfloat16),
            jax.ShapeDtypeStruct((count, width), jnp.bfloat16),
        ],
        input_output_aliases={len(inputs): 0} if earlier else {},
        compiler_params=pltpu.CompilerParams(vmem_limit_bytes=62 * 1024 * 1024),
        cost_estimate=pl.CostEstimate(
            flops=rows * cache * HD * 8,
            bytes_accessed=cache * HD * 4,
            transcendentals=rows * cache,
        ),
        name="attention",
    )(*inputs, *earlier)


def home_kernel(place_ref, residual_ref, *refs):
    pieces, out_ref = refs[:Y], refs[Y]
    width = pieces[0].shape[1]
    for q, piece in enumerate(pieces):
        columns = pl.ds(pl.multiple_of(place_ref[q] * width, width), width)
        out_ref[:, columns] = (
            residual_ref[:, columns].astype(jnp.float32) + piece[...].astype(jnp.float32)
        ).astype(out_ref.dtype)


def in_columns(kernel, places, arrays, rows):
    return pl.pallas_call(
        kernel,
        in_specs=[pl.BlockSpec(memory_space=pltpu.SMEM)]
        + [pl.BlockSpec(memory_space=pltpu.VMEM)] * len(arrays),
        out_specs=pl.BlockSpec(memory_space=pltpu.VMEM),
        out_shape=jax.ShapeDtypeStruct((rows, Y * arrays[-1].shape[1]), jnp.bfloat16),
        cost_estimate=pl.CostEstimate(
            flops=rows * 1024, bytes_accessed=rows * 4096, transcendentals=0
        ),
    )(places, *arrays)


def owner_kernel(want_ref, come_ref, *refs):
    blocks, outs = refs[:Z], refs[Z:]
    for r, out in enumerate(outs):
        for d, block in enumerate(blocks):

            @pl.when(want_ref[r] == d)
            def _():
                out[...] = (
                    block[...].astype(jnp.float32) + come_ref[d // 2].astype(jnp.float32)
                ).astype(out.dtype)


def owner_sums(blocks, come, want):
    shape = come.shape[1:]
    first = pl.BlockSpec(shape, lambda i: (0, 0))
    return pl.pallas_call(
        owner_kernel,
        grid=(1,),
        in_specs=[pl.BlockSpec(memory_space=pltpu.SMEM)]
        + [pl.BlockSpec(come.shape, lambda i: (0, 0, 0))]
        + [first] * Z,
        out_specs=[first] * X,
        out_shape=[jax.ShapeDtypeStruct(shape, jnp.float32)]
        + [jax.ShapeDtypeStruct(shape, jnp.bfloat16)] * (X - 1),
        cost_estimate=pl.CostEstimate(
            flops=blocks[0].size * X, bytes_accessed=blocks[0].size * 24, transcendentals=0
        ),
        name="owner_sums",
    )(want, come, *blocks)


def gather_kernel(*refs):
    pieces, all_ref = refs[:Y], refs[Y]
    rows = NODES * pieces[0].shape[0] // (NODES + ACC)
    count = pieces[0].shape[0] - rows
    for q, piece in enumerate(pieces):
        all_ref[q * rows : (q + 1) * rows] = piece[:rows]
        all_ref[Y * rows + q * count : Y * rows + (q + 1) * count] = piece[rows:]


def gather_rows(pieces):
    size, width = pieces[0].shape
    return pl.pallas_call(
        gather_kernel,
        in_specs=[pl.BlockSpec(memory_space=pltpu.VMEM)] * Y,
        out_specs=pl.BlockSpec(memory_space=pltpu.VMEM),
        out_shape=jax.ShapeDtypeStruct((Y * size, width), jnp.bfloat16),
        cost_estimate=pl.CostEstimate(
            flops=Y * size * width, bytes_accessed=Y * size * width * 4, transcendentals=0
        ),
        name="gather_rows",
    )(*pieces)


def spread_kernel(at_ref, *refs):
    blocks, out_ref = refs[:Z], refs[Z]
    count = out_ref.shape[1]
    for d, block in enumerate(blocks):
        for q in range(Y):
            place = (at_ref[1] + Y - q) % Y * Z + (at_ref[0] + d) % Z
            out_ref[place] = block[q * count : (q + 1) * count, :]


def spread(blocks, at):
    size, width = blocks[0].shape
    few = size * ACC // (NODES + ACC)
    count = few // Y
    last = pl.BlockSpec((few, width), lambda i: (size // few - 1, 0))
    return pl.pallas_call(
        spread_kernel,
        grid=(1,),
        in_specs=[pl.BlockSpec(memory_space=pltpu.SMEM)] + [last] * Z,
        out_specs=pl.BlockSpec((Y * Z, count, width), lambda i: (0, 0, 0)),
        out_shape=jax.ShapeDtypeStruct((Y * Z, count, width), blocks[0].dtype),
        cost_estimate=pl.CostEstimate(
            flops=count * width, bytes_accessed=Z * Y * count * width * 4, transcendentals=0
        ),
        name="spread",
    )(at, *blocks)


def tile_kernel(accepted_ref, residual_ref, parts_ref, out_ref):
    requests, count = accepted_ref.shape
    nodes = residual_ref.shape[0] // requests
    width = parts_ref.shape[2]
    for r in range(requests):
        hot = lax.broadcasted_iota(jnp.int32, (nodes, count), 0) == accepted_ref[r : r + 1, :]
        kept = lax.dot_general(
            hot.astype(jnp.float32).astype(jnp.bfloat16),
            residual_ref[r * nodes : (r + 1) * nodes, :],
            (((0,), (0,)), ((), ())),
            preferred_element_type=jnp.float32,
        )
        took = slice(r * count, (r + 1) * count)
        for s in range(Y):
            total = kept[:, s * width : (s + 1) * width]
            for j in range(Z):
                total = total + parts_ref[s * Z + j, took].astype(jnp.float32)
            for copy in range(out_ref.shape[0]):
                out_ref[copy, took, s * width : (s + 1) * width] = total.astype(out_ref.dtype)


def accepted_tile(residual, accepted_nodes, parts, copies):
    count, width = parts.shape[1:]
    return pl.pallas_call(
        tile_kernel,
        in_specs=[pl.BlockSpec(memory_space=pltpu.VMEM)] * 3,
        out_specs=pl.BlockSpec(memory_space=pltpu.VMEM),
        out_shape=jax.ShapeDtypeStruct((copies, count, Y * width), residual.dtype),
        cost_estimate=pl.CostEstimate(
            flops=residual.size * 64, bytes_accessed=residual.size * 10, transcendentals=0
        ),
        name="accepted_tile",
    )(accepted_nodes, residual, parts)


def device(z, y, j):
    return (z * Y + y) * X * C + j


def shift_z(value, by):
    pairs = [(z * Y + y, (z + by) % Z * Y + y) for z in range(Z) for y in range(Y)]
    return lax.ppermute(value, "dp", pairs)


def shift_y(value, by):
    pairs = [(z * Y + y, z * Y + (y + by) % Y) for z in range(Z) for y in range(Y)]
    return lax.ppermute(value, "dp", pairs)


def shift_x(value, by):
    pairs = [(x * C + c, (x + by) % X * C + c) for x in range(X) for c in range(C)]
    return lax.ppermute(value, "mp", pairs)


def swap_core(value):
    return lax.ppermute(value, "mp", [(j, j ^ 1) for j in range(X * C)])


def per_device(
    queries,
    tree_keys,
    tree_values,
    cache_keys,
    cache_values,
    cache_lens,
    parents,
    accepted_nodes,
    residual,
    out_weight,
):
    dp, mp = lax.axis_index("dp"), lax.axis_index("mp")
    z, y, x, c = dp // Y, dp % Y, mp // C, mp % C
    requests, nodes = parents.shape
    rows = requests * nodes
    count = requests * accepted_nodes.shape[1]
    inner, width = out_weight.shape
    f32, bf16 = jnp.float32, jnp.bfloat16

    weights = [out_weight] + [None] * (Z - 1)
    ahead = behind = out_weight
    for d in range(1, Z // 2):
        ahead, behind = shift_z(ahead, -1), shift_z(behind, 1)
        weights[d], weights[Z - d] = ahead, behind
    half = inner // 2
    low, high = shift_z(ahead[:half], -1), shift_z(behind[half:], 1)

    inputs = (
        cache_lens,
        parents,
        queries,
        tree_keys,
        tree_values,
        cache_keys,
        cache_values,
        accepted_nodes,
    )
    earlier, picks = (), []
    for r in range(requests):
        attended, picked = attention(r, earlier, inputs)
        earlier = (attended,)
        picks.append(picked)
    packed = jnp.concatenate([attended, *picks], axis=0)
    packed = [packed] + [shift_y(packed, q) for q in range(1, Y)]
    gathered = gather_rows(packed)

    def partial(value, d):
        if d != Z // 2:
            total = jnp.dot(value, weights[d], preferred_element_type=f32)
        else:
            total = jnp.dot(value[:, :half], low, preferred_element_type=f32)
            total = total + jnp.dot(value[:, half:], high, preferred_element_type=f32)
        return total.astype(bf16)

    blocks = []
    for d in range(Z):
        blocks.append(partial(gathered, d))
    few = spread(blocks, jnp.stack([z, y]))
    planes = [
        [device(zz, yy, j) for yy in range(Y) for j in range(X * C)] for zz in range(Z)
    ]
    few = lax.all_to_all(few, ("dp", "mp"), 0, 0, axis_index_groups=planes, tiled=True)
    tiles = accepted_tile(residual, accepted_nodes, few, Z * Y)
    accepted_hidden = lax.all_to_all(tiles, "dp", 0, 0, tiled=True)
    accepted_hidden = accepted_hidden.reshape(Z * Y * count, Y * width)

    odd = (z + c) % 2
    come = swap_core(
        jnp.stack(
            [
                jnp.where(odd == 0, blocks[2 * e + 1], blocks[2 * e])[: Y * rows]
                for e in range(X)
            ]
        ),
    )
    want = (x + jnp.arange(X) - (z + odd) // 2) % X * 2 + odd
    own, *sent = owner_sums(blocks, come, want)
    for by in range(1, X):
        own = own + shift_x(sent[by - 1], by).astype(f32)
    own = own.astype(bf16)
    home = [own[:rows]] + [shift_y(own[q * rows : (q + 1) * rows], -q) for q in range(1, Y)]
    places = (y + jnp.arange(Y)) % Y
    tree_hidden = in_columns(home_kernel, places, [residual] + home, rows)
    return (tree_hidden, accepted_hidden)


def solution(mesh):
    placed = (
        P("dp", "mp"),
        P("dp", "mp"),
        P("dp", "mp"),
        P("dp", None, "mp"),
        P("dp", None, "mp"),
        P("dp"),
        P("dp", None),
        P("dp", None),
        P("dp", "mp"),
        P("mp", "dp"),
    )

    return jax.shard_map(
        per_device,
        mesh=mesh,
        in_specs=placed,
        out_specs=(P("dp", "mp"), P(None, "mp")),
        check_vma=False,
    )
```

time: 196 us -> 147 us (0.75)
  waiting for transfers between devices: 74.6 us -> 52 us
  starting transfers between devices: 67 us -> 45.1 us
  local copies, waits for them, and re-layouts: 9.93 us -> 6.6 us
  Pallas kernels: 25.7 us -> 28 us
  other arithmetic: 6.13 us -> 3.83 us
    ppermute x22 -> x8, starting transfers between devices: 41.5 us -> 16.6 us  [shift_z(): return lax.ppermute(value, 'dp', pairs)]
    ppermute x22 -> x8, waiting for transfers between devices: 42.7 us -> 20.5 us  [shift_z(): return lax.ppermute(value, 'dp', pairs)]
    ppermute x12 -> x6, waiting for transfers between devices: 25.2 us -> 8.73 us  [shift_y(): return lax.ppermute(value, 'dp', pairs)]
    all_to_all x1 -> x2, starting transfers between devices: 4.32 us -> 16.8 us  [the longest x1 8.99 us: per_device(): lax.all_to_all(few, ('dp', 'mp'), 0, 0, axis_index_groups=planes, tiled=T...]
    ppermute x3, waiting for transfers between devices: 5.74 us -> 14.1 us  [shift_x(): return lax.ppermute(value, 'mp', pairs)]
    ppermute x12 -> x6, starting transfers between devices: 16.7 us -> 8.68 us  [shift_y(): return lax.ppermute(value, 'dp', pairs)]
    all_to_all x1 -> x2, waiting for transfers between devices: 1 us -> 6.63 us  [the longest x1 6.62 us: per_device(): lax.all_to_all(few, ('dp', 'mp'), 0, 0, axis_index_groups=planes, tiled=T...]
    gather x2 -> x0, local copies, waits for them, and re-layouts: 3.19 us -> none  [the longest x1 1.59 us: per_device(): jnp.take(residual, node_rows, axis=0)]
  transfers between devices with their start and end apart: 40 -> 20, of which waited for: 19 -> 13; matrix products, arithmetic and copies ran while one was open for 9% -> 8% of each run, Pallas kernels for 4% -> 5%
where the time goes in v1:
time: 147 us; the launch traced here: 145 us
  waiting for transfers between devices  52 us (35%)
  starting transfers between devices  45.1 us (31%)
  Pallas kernels  28 us (19%)
  matrix products  8.18 us (6%)
  local copies, waits for them, and re-layouts  6.6 us (4%)
  other arithmetic  3.83 us (3%)
    ppermute x8, waiting for transfers between devices, shift_z(): return lax.ppermute(value, 'dp', pairs)  20.5 us
    ppermute x8, starting transfers between devices, shift_z(): return lax.ppermute(value, 'dp', pairs)  16.6 us
    pallas_call x2, Pallas kernels, attention(): pl.pallas_call(functools.partial(attention_kernel, request=request), grid...  16.4 us
    ppermute x3, waiting for transfers between devices, shift_x(): return lax.ppermute(value, 'mp', pairs)  14.1 us
    all_to_all x1, starting transfers between devices, per_device(): lax.all_to_all(few, ('dp', 'mp'), 0, 0, axis_index_groups=planes, tiled=T...  8.99 us
    ppermute x6, waiting for transfers between devices, shift_y(): return lax.ppermute(value, 'dp', pairs)  8.73 us
    ppermute x6, starting transfers between devices, shift_y(): return lax.ppermute(value, 'dp', pairs)  8.68 us
    all_to_all x1, starting transfers between devices, per_device(): accepted_hidden = lax.all_to_all(tiles, 'dp', 0, 0, tiled=True)  7.83 us
  transfers between devices with their start and end apart: 20, of which 13 were waited for; matrix products, arithmetic and copies ran while one was open for 8% of the time, Pallas kernels for 5%

profile of v1, /device:TPU:8, one launch (start us, length us, event | category | flops | bytes accessed | tf_op | source)
XLA Modules:
  0.0 144.6 jit_solution(2262938633932177879)
XLA Ops:
  0.6 8.1 %attention.2 = (bf16[128,1024]{1,0:T(8,128)(2,1)}, bf16[8,1024]{1,0:T(8,128)(2,1)}) custom-call(s32[2]{0:T(128)} %lens_ref.3, s32[2,64]{1,0:T(2,128)} %parents_ref.3, bf16[128,1024]{1,0:T(8,128)(2,1)} %q_ref.3, bf16[128,128]{1,0:T(8,128)(2,1)} %tk_ref.3, bf16[128,128]{1,0:T(8,128)(2,1)} %tv_ref.3, bf16[2,4096,128]{2,1,0:T(8,128)(2,1)} %k_ref.3, ...), custom_call_target="tpu_custom_call" | custom-call | flops 2147483648 | bytes 2097152 | tf_op jit(solution)/shard_map/attention/pallas_call | solution.py:107
  8.7 8.3 %attention.3 = (bf16[128,1024]{1,0:T(8,128)(2,1)}, bf16[8,1024]{1,0:T(8,128)(2,1)}) custom-call(s32[2]{0:T(128)} %lens_ref.3, s32[2,64]{1,0:T(2,128)} %parents_ref.3, bf16[128,1024]{1,0:T(8,128)(2,1)} %q_ref.3, bf16[128,128]{1,0:T(8,128)(2,1)} %tk_ref.3, bf16[128,128]{1,0:T(8,128)(2,1)} %tv_ref.3, ...), custom_call_target="tpu_custom_call", output_to_operand_aliasing={{0}: (8, {})} | custom-call | flops 2147483648 | bytes 2097152 | tf_op jit(solution)/shard_map/attention/pallas_call | solution.py:107
  18.7 2.3 %collective-permute-start.1 = (bf16[144,1024]{1,0:T(8,128)(2,1)S(1)}, bf16[144,1024]{1,0:T(8,128)(2,1)S(1)}, u32[]{:S(2)}, u32[]{:S(2)}) collective-permute-start(bf16[144,1024]{1,0:T(8,128)(2,1)S(1)} %constant_dynamic-update-slice_fusion.refs_0_), channel_id=1, source_target_pairs={{0,16},{8,24},{16,0},{24,8},{32,48},{40,56},{48,32},{56,40},{64,80... | collective-permute-start | bytes 884744 | tf_op jit(solution)/shard_map/ppermute | solution.py:296
  21.0 1.7 %collective-permute-start.2 = (bf16[144,1024]{1,0:T(8,128)(2,1)S(1)}, bf16[144,1024]{1,0:T(8,128)(2,1)S(1)}, u32[]{:S(2)}, u32[]{:S(2)}) collective-permute-start(bf16[144,1024]{1,0:T(8,128)(2,1)S(1)} %constant_dynamic-update-slice_fusion.refs_0_), channel_id=1, source_target_pairs={{0,24},{8,0},{16,8},{24,16},{32,56},{40,32},{48,40},{56,48},{64,88... | collective-permute-start | bytes 884744 | tf_op jit(solution)/shard_map/ppermute | solution.py:296
  23.7 3.9 %collective-permute-start.3 = (bf16[1024,256]{1,0:T(8,128)(2,1)S(1)}, bf16[1024,256]{1,0:T(8,128)(2,1)S(1)}, u32[]{:S(2)}, u32[]{:S(2)}) collective-permute-start(bf16[1024,256]{1,0:T(8,128)(2,1)S(1)} %copy-done.20), channel_id=1, source_target_pairs={{0,224},{8,232},{16,240},{24,248},{32,0},{40,8},{48,16},{56,24},{6... | collective-permute-start | bytes 1572872 | tf_op jit(solution)/shard_map/ppermute | solution.py:291
  28.6 1.5 %collective-permute-done.1.refs_2_ = bf16[144,1024]{1,0:T(8,128)(2,1)S(1)} collective-permute-done((bf16[144,1024]{1,0:T(8,128)(2,1)S(1)}, bf16[144,1024]{1,0:T(8,128)(2,1)S(1)}, u32[]{:S(2)}, u32[]{:S(2)}) %collective-permute-start.1) | collective-permute-done | bytes 294944 | tf_op jit(solution)/shard_map/ppermute | solution.py:296
  30.1 4.9 %collective-permute-done.2.refs_3_ = bf16[144,1024]{1,0:T(8,128)(2,1)S(1)} collective-permute-done((bf16[144,1024]{1,0:T(8,128)(2,1)S(1)}, bf16[144,1024]{1,0:T(8,128)(2,1)S(1)}, u32[]{:S(2)}, u32[]{:S(2)}) %collective-permute-start.2) | collective-permute-done | bytes 294944 | tf_op jit(solution)/shard_map/ppermute | solution.py:296
  35.7 2.3 %gather_rows.1 = bf16[576,1024]{1,0:T(8,128)(2,1)} custom-call(bf16[144,1024]{1,0:T(8,128)(2,1)} %copy-done.9, bf16[144,1024]{1,0:T(8,128)(2,1)} %copy-done.13, bf16[144,1024]{1,0:T(8,128)(2,1)} %copy-done.14, bf16[144,1024]{1,0:T(8,128)(2,1)} %copy-done.15), custom_call_target="tpu_custom_call" | custom-call | flops 589824 | bytes 2359296 | tf_op jit(solution)/shard_map/gather_rows/pallas_call | solution.py:211
  38.1 1.8 %convolution_convert_fusion.5.refs_0_ = bf16[576,256]{1,0:T(8,128)(2,1)S(1)} fusion(bf16[576,1024]{1,0:T(8,128)(2,1)} %gather_rows.1, bf16[1024,256]{1,0:T(8,128)(2,1)S(1)} %copy-done.20), kind=kOutput, calls=%fused_computation.7 | convolution fusion | flops 302137344 | bytes 1998848 | tf_op jit(solution)/shard_map/dot_general | solution.py:357
  39.9 2.0 %collective-permute-start.7 = (bf16[1024,256]{1,0:T(8,128)(2,1)S(1)}, bf16[1024,256]{1,0:T(8,128)(2,1)S(1)}, u32[]{:S(2)}, u32[]{:S(2)}) collective-permute-start(bf16[1024,256]{1,0:T(8,128)(2,1)S(1)} %collective-permute-done.6), channel_id=1, source_target_pairs={{0,32},{8,40},{16,48},{24,56},{32,64},{40,72},{48,80},{56,88},{64,... | collective-permute-start | bytes 1572872 | tf_op jit(solution)/shard_map/ppermute | solution.py:291
  41.9 3.0 %collective-permute-start.4 = (bf16[1024,256]{1,0:T(8,128)(2,1)S(1)}, bf16[1024,256]{1,0:T(8,128)(2,1)S(1)}, u32[]{:S(2)}, u32[]{:S(2)}) collective-permute-start(bf16[1024,256]{1,0:T(8,128)(2,1)S(1)} %collective-permute-done.3), channel_id=1, source_target_pairs={{0,224},{8,232},{16,240},{24,248},{32,0},{40,8},{48,16},{56,24},{6... | collective-permute-start | bytes 1572872 | tf_op jit(solution)/shard_map/ppermute | solution.py:291
  46.0 10.0 %collective-permute-done.7 = bf16[1024,256]{1,0:T(8,128)(2,1)S(1)} collective-permute-done((bf16[1024,256]{1,0:T(8,128)(2,1)S(1)}, bf16[1024,256]{1,0:T(8,128)(2,1)S(1)}, u32[]{:S(2)}, u32[]{:S(2)}) %collective-permute-start.7) | collective-permute-done | bytes 524320 | tf_op jit(solution)/shard_map/ppermute | solution.py:291
  56.1 3.2 %collective-permute-start.5 = (bf16[1024,256]{1,0:T(8,128)(2,1)S(1)}, bf16[1024,256]{1,0:T(8,128)(2,1)S(1)}, u32[]{:S(2)}, u32[]{:S(2)}) collective-permute-start(bf16[1024,256]{1,0:T(8,128)(2,1)S(1)} %collective-permute-done.4), channel_id=1, source_target_pairs={{0,224},{8,232},{16,240},{24,248},{32,0},{40,8},{48,16},{56,24},{6... | collective-permute-start | bytes 1572872 | tf_op jit(solution)/shard_map/ppermute | solution.py:291
  61.0 8.8 %collective-permute-done.8 = bf16[1024,256]{1,0:T(8,128)(2,1)S(1)} collective-permute-done((bf16[1024,256]{1,0:T(8,128)(2,1)S(1)}, bf16[1024,256]{1,0:T(8,128)(2,1)S(1)}, u32[]{:S(2)}, u32[]{:S(2)}) %collective-permute-start.8) | collective-permute-done | bytes 524320 | tf_op jit(solution)/shard_map/ppermute | solution.py:291
  69.9 3.5 %collective-permute-start.9 = (bf16[512,256]{1,0:T(8,128)(2,1)S(1)}, bf16[512,256]{1,0:T(8,128)(2,1)S(1)}, u32[]{:S(2)}, u32[]{:S(2)}) collective-permute-start(bf16[512,256]{1,0:T(8,128)(2,1)S(1)} %slice.53), channel_id=1, source_target_pairs={{0,224},{8,232},{16,240},{24,248},{32,0},{40,8},{48,16},{56,24},{6... | collective-permute-start | bytes 786440 | tf_op jit(solution)/shard_map/ppermute | solution.py:291
  73.4 1.2 convolution_convert_fusion.2.refs_5_
  75.8 1.7 %collective-permute-done.10 = bf16[512,256]{1,0:T(8,128)(2,1)S(1)} collective-permute-done((bf16[512,256]{1,0:T(8,128)(2,1)S(1)}, bf16[512,256]{1,0:T(8,128)(2,1)S(1)}, u32[]{:S(2)}, u32[]{:S(2)}) %collective-permute-start.10) | collective-permute-done | bytes 262176 | tf_op jit(solution)/shard_map/ppermute | solution.py:291
  78.9 1.7 %spread.1 = bf16[32,16,256]{2,1,0:T(8,128)(2,1)} custom-call(s32[2]{0:T(128)} %pad_add_fusion.at_ref, bf16[576,256]{1,0:T(8,128)(2,1)} %copy-done.2, bf16[576,256]{1,0:T(8,128)(2,1)} %copy-done.3, bf16[576,256]{1,0:T(8,128)(2,1)} %convolution_convert_fusion.3.refs_2_, bf16[576,256]{1,0:T(8,128)(2,1)} %convolution_convert_fusion.4.refs_3_, ...), custom_call_target="tpu_custom_call" | custom-call | flops 4096 | bytes 524288 | tf_op jit(solution)/shard_map/spread/pallas_call | solution.py:237
  80.6 9.0 %all-to-all-start = ((bf16[32,16,256]{2,1,0:T(8,128)(2,1)}), bf16[32,16,256]{2,1,0:T(8,128)(2,1)S(1)}, u32[]{:S(2)}, u32[]{:S(2)}) async-start(bf16[32,16,256]{2,1,0:T(8,128)(2,1)} %spread.1), calls=%async_computation | async-start | bytes 524288 | tf_op jit(solution)/shard_map/all_to_all | solution.py:370
  90.4 6.6 %all-to-all-done.parts_ref = bf16[32,16,256]{2,1,0:T(8,128)(2,1)S(1)} async-done(((bf16[32,16,256]{2,1,0:T(8,128)(2,1)}), bf16[32,16,256]{2,1,0:T(8,128)(2,1)S(1)}, u32[]{:S(2)}, u32[]{:S(2)}) %all-to-all-start) | async-done | bytes 262176 | tf_op jit(solution)/shard_map/all_to_all | solution.py:370
  97.7 2.4 %accepted_tile.1 = bf16[32,16,1024]{2,1,0:T(8,128)(2,1)} custom-call(s32[2,8]{1,0:T(2,128)} %accepted_ref.5, bf16[128,1024]{1,0:T(8,128)(2,1)} %residual_ref.3, bf16[32,16,256]{2,1,0:T(8,128)(2,1)} %copy-done.11), custom_call_target="tpu_custom_call" | custom-call | flops 8388608 | bytes 1310720 | tf_op jit(solution)/shard_map/accepted_tile/pallas_call | solution.py:273
  100.1 7.8 %all-to-all-start.1 = ((bf16[32,16,1024]{2,1,0:T(8,128)(2,1)}), bf16[32,16,1024]{2,1,0:T(8,128)(2,1)S(1)}, u32[]{:S(2)}, u32[]{:S(2)}) async-start(bf16[32,16,1024]{2,1,0:T(8,128)(2,1)} %accepted_tile.1), calls=%async_computation.1 | async-start | bytes 2097152 | tf_op jit(solution)/shard_map/all_to_all | solution.py:372
  108.8 2.0 %collective-permute-done.11.come_ref = bf16[4,512,256]{2,1,0:T(8,128)(2,1)S(1)} collective-permute-done((bf16[4,512,256]{2,1,0:T(8,128)(2,1)S(1)}, bf16[4,512,256]{2,1,0:T(8,128)(2,1)S(1)}, u32[]{:S(2)}, u32[]{:S(2)}) %collective-permute-start.11) | collective-permute-done | bytes 1048608 | tf_op jit(solution)/shard_map/ppermute | solution.py:305
  111.8 3.4 %owner_sums.1 = (f32[512,256]{1,0:T(8,128)}, bf16[512,256]{1,0:T(8,128)(2,1)}, bf16[512,256]{1,0:T(8,128)(2,1)}, bf16[512,256]{1,0:T(8,128)(2,1)}) custom-call(s32[4]{0:T(128)} %fusion.9.want_ref, bf16[4,512,256]{2,1,0:T(8,128)(2,1)} %copy-done.10, bf16[576,256]{1,0:T(8,128)(2,1)} %copy-done.2, bf16[576,256]{1,0:T(8,128)(2,1)} %copy-done.3, ...), custom_call_target="tpu_custom_call" | custom-call | flops 589824 | bytes 3538944 | tf_op jit(solution)/shard_map/owner_sums/pallas_call | solution.py:184
  115.2 1.6 %collective-permute-start.14 = (bf16[512,256]{1,0:T(8,128)(2,1)}, bf16[512,256]{1,0:T(8,128)(2,1)S(1)}, u32[]{:S(2)}, u32[]{:S(2)}) collective-permute-start(bf16[512,256]{1,0:T(8,128)(2,1)} %get-tuple-element.17), channel_id=1, source_target_pairs={{0,6},{1,7},{2,0},{3,1},{4,2},{5,3},{6,4},{7,5},{8,14},{9,15},{10,... | collective-permute-start | bytes 786440 | tf_op jit(solution)/shard_map/ppermute | solution.py:301
  116.8 1.3 collective-permute-start.13
  118.0 6.5 %collective-permute-done.14 = bf16[512,256]{1,0:T(8,128)(2,1)S(1)} collective-permute-done((bf16[512,256]{1,0:T(8,128)(2,1)}, bf16[512,256]{1,0:T(8,128)(2,1)S(1)}, u32[]{:S(2)}, u32[]{:S(2)}) %collective-permute-start.14) | collective-permute-done | bytes 262176 | tf_op jit(solution)/shard_map/ppermute | solution.py:301
  124.5 3.2 %collective-permute-done.13 = bf16[512,256]{1,0:T(8,128)(2,1)S(1)} collective-permute-done((bf16[512,256]{1,0:T(8,128)(2,1)}, bf16[512,256]{1,0:T(8,128)(2,1)S(1)}, u32[]{:S(2)}, u32[]{:S(2)}) %collective-permute-start.13) | collective-permute-done | bytes 262176 | tf_op jit(solution)/shard_map/ppermute | solution.py:301
  127.7 4.5 %collective-permute-done.12 = bf16[512,256]{1,0:T(8,128)(2,1)S(1)} collective-permute-done((bf16[512,256]{1,0:T(8,128)(2,1)}, bf16[512,256]{1,0:T(8,128)(2,1)S(1)}, u32[]{:S(2)}, u32[]{:S(2)}) %collective-permute-start.12) | collective-permute-done | bytes 262176 | tf_op jit(solution)/shard_map/ppermute | solution.py:301
  134.2 2.7 %collective-permute-start.16 = (bf16[128,256]{1,0:T(8,128)(2,1)S(1)}, bf16[128,256]{1,0:T(8,128)(2,1)S(1)}, u32[]{:S(2)}, u32[]{:S(2)}) collective-permute-start(bf16[128,256]{1,0:T(8,128)(2,1)S(1)} %get-tuple-element.19), channel_id=1, source_target_pairs={{0,16},{8,24},{16,0},{24,8},{32,48},{40,56},{48,32},{56,40},{64,80... | collective-permute-start | bytes 196616 | tf_op jit(solution)/shard_map/ppermute | solution.py:296
  136.9 1.8 %collective-permute-start.17 = (bf16[128,256]{1,0:T(8,128)(2,1)S(1)}, bf16[128,256]{1,0:T(8,128)(2,1)S(1)}, u32[]{:S(2)}, u32[]{:S(2)}) collective-permute-start(bf16[128,256]{1,0:T(8,128)(2,1)S(1)} %get-tuple-element.18), channel_id=1, source_target_pairs={{0,8},{8,16},{16,24},{24,0},{32,40},{40,48},{48,56},{56,32},{64,72... | collective-permute-start | bytes 196616 | tf_op jit(solution)/shard_map/ppermute | solution.py:296
  141.8 1.8 %shard_map.113 = bf16[128,1024]{1,0:T(8,128)(2,1)} custom-call(s32[4]{0:T(128)} %and_select_fusion.1.place_ref, bf16[128,1024]{1,0:T(8,128)(2,1)} %residual_ref.3, bf16[128,256]{1,0:T(8,128)(2,1)} %get-tuple-element.21.refs_0_, bf16[128,256]{1,0:T(8,128)(2,1)} %copy-done.16, bf16[128,256]{1,0:T(8,128)(2,1)} %copy-done.17, bf16[128,256]{1,0:T(8,128)(2,1)} %copy-done.18), custom_call_target="tpu_custom_call" | custom-call | flops 131072 | bytes 524288 | tf_op jit(solution)/shard_map/pallas_call | solution.py:157
  (82 shorter events, 19.4 us)
Async XLA Ops:
  8.7 9.2 %copy-start.19 = (bf16[8,1024]{1,0:T(8,128)(2,1)S(1)}, bf16[8,1024]{1,0:T(8,128)(2,1)}, u32[]{:S(2)}) copy-start(bf16[8,1024]{1,0:T(8,128)(2,1)} %get-tuple-element.12) | copy-start | bytes 49156
  8.7 14.0 %copy-start.20 = (bf16[1024,256]{1,0:T(8,128)(2,1)S(1)}, bf16[1024,256]{1,0:T(8,128)(2,1)}, u32[]{:S(2)}) copy-start(bf16[1024,256]{1,0:T(8,128)(2,1)} %param.19) | copy-start | bytes 1572868
  18.7 16.3 %copy-start.9 = (bf16[144,1024]{1,0:T(8,128)(2,1)}, bf16[144,1024]{1,0:T(8,128)(2,1)S(1)}, u32[]{:S(2)}) copy-start(bf16[144,1024]{1,0:T(8,128)(2,1)S(1)} %constant_dynamic-update-slice_fusion.refs_0_) | copy-start | bytes 884740
  18.7 9.9 %collective-permute-start = (bf16[144,1024]{1,0:T(8,128)(2,1)S(1)}, bf16[144,1024]{1,0:T(8,128)(2,1)S(1)}, u32[]{:S(2)}, u32[]{:S(2)}) collective-permute-start(bf16[144,1024]{1,0:T(8,128)(2,1)S(1)} %constant_dynamic-update-slice_fusion.refs_0_), channel_id=1, source_target_pairs={{0,8},{8,16},{16,24},{24,0},{32,40},{40,48},{48,56},{56,32},{64,72... | collective-permute-start | bytes 884744 | tf_op jit(solution)/shard_map/ppermute | solution.py:296
  18.7 11.4 %collective-permute-start.1 = (bf16[144,1024]{1,0:T(8,128)(2,1)S(1)}, bf16[144,1024]{1,0:T(8,128)(2,1)S(1)}, u32[]{:S(2)}, u32[]{:S(2)}) collective-permute-start(bf16[144,1024]{1,0:T(8,128)(2,1)S(1)} %constant_dynamic-update-slice_fusion.refs_0_), channel_id=1, source_target_pairs={{0,16},{8,24},{16,0},{24,8},{32,48},{40,56},{48,32},{56,40},{64,80... | collective-permute-start | bytes 884744 | tf_op jit(solution)/shard_map/ppermute | solution.py:296
  21.0 14.0 %collective-permute-start.2 = (bf16[144,1024]{1,0:T(8,128)(2,1)S(1)}, bf16[144,1024]{1,0:T(8,128)(2,1)S(1)}, u32[]{:S(2)}, u32[]{:S(2)}) collective-permute-start(bf16[144,1024]{1,0:T(8,128)(2,1)S(1)} %constant_dynamic-update-slice_fusion.refs_0_), channel_id=1, source_target_pairs={{0,24},{8,0},{16,8},{24,16},{32,56},{40,32},{48,40},{56,48},{64,88... | collective-permute-start | bytes 884744 | tf_op jit(solution)/shard_map/ppermute | solution.py:296
  22.7 17.2 %collective-permute-start.6 = (bf16[1024,256]{1,0:T(8,128)(2,1)S(1)}, bf16[1024,256]{1,0:T(8,128)(2,1)S(1)}, u32[]{:S(2)}, u32[]{:S(2)}) collective-permute-start(bf16[1024,256]{1,0:T(8,128)(2,1)S(1)} %copy-done.20), channel_id=1, source_target_pairs={{0,32},{8,40},{16,48},{24,56},{32,64},{40,72},{48,80},{56,88},{64,... | collective-permute-start | bytes 1572872 | tf_op jit(solution)/shard_map/ppermute | solution.py:291
  23.7 18.2 %collective-permute-start.3 = (bf16[1024,256]{1,0:T(8,128)(2,1)S(1)}, bf16[1024,256]{1,0:T(8,128)(2,1)S(1)}, u32[]{:S(2)}, u32[]{:S(2)}) collective-permute-start(bf16[1024,256]{1,0:T(8,128)(2,1)S(1)} %copy-done.20), channel_id=1, source_target_pairs={{0,224},{8,232},{16,240},{24,248},{32,0},{40,8},{48,16},{56,24},{6... | collective-permute-start | bytes 1572872 | tf_op jit(solution)/shard_map/ppermute | solution.py:291
  28.6 6.4 %copy-start.13 = (bf16[144,1024]{1,0:T(8,128)(2,1)}, bf16[144,1024]{1,0:T(8,128)(2,1)S(1)}, u32[]{:S(2)}) copy-start(bf16[144,1024]{1,0:T(8,128)(2,1)S(1)} %collective-permute-done.refs_1_) | copy-start | bytes 884740
  38.1 6.8 %copy-start = (bf16[576,1024]{1,0:T(8,128)(2,1)S(1)}, bf16[576,1024]{1,0:T(8,128)(2,1)}, u32[]{:S(2)}) copy-start(bf16[576,1024]{1,0:T(8,128)(2,1)} %gather_rows.1) | copy-start | bytes 3538948
  39.9 16.1 %collective-permute-start.7 = (bf16[1024,256]{1,0:T(8,128)(2,1)S(1)}, bf16[1024,256]{1,0:T(8,128)(2,1)S(1)}, u32[]{:S(2)}, u32[]{:S(2)}) collective-permute-start(bf16[1024,256]{1,0:T(8,128)(2,1)S(1)} %collective-permute-done.6), channel_id=1, source_target_pairs={{0,32},{8,40},{16,48},{24,56},{32,64},{40,72},{48,80},{56,88},{64,... | collective-permute-start | bytes 1572872 | tf_op jit(solution)/shard_map/ppermute | solution.py:291
  41.9 14.2 %collective-permute-start.4 = (bf16[1024,256]{1,0:T(8,128)(2,1)S(1)}, bf16[1024,256]{1,0:T(8,128)(2,1)S(1)}, u32[]{:S(2)}, u32[]{:S(2)}) collective-permute-start(bf16[1024,256]{1,0:T(8,128)(2,1)S(1)} %collective-permute-done.3), channel_id=1, source_target_pairs={{0,224},{8,232},{16,240},{24,248},{32,0},{40,8},{48,16},{56,24},{6... | collective-permute-start | bytes 1572872 | tf_op jit(solution)/shard_map/ppermute | solution.py:291
  46.0 32.8 %copy-start.4 = (bf16[576,256]{1,0:T(8,128)(2,1)}, bf16[576,256]{1,0:T(8,128)(2,1)S(1)}, u32[]{:S(2)}) copy-start(bf16[576,256]{1,0:T(8,128)(2,1)S(1)} %convolution_convert_fusion.1.refs_7_) | copy-start | bytes 884740
  56.1 13.7 %collective-permute-start.8 = (bf16[1024,256]{1,0:T(8,128)(2,1)S(1)}, bf16[1024,256]{1,0:T(8,128)(2,1)S(1)}, u32[]{:S(2)}, u32[]{:S(2)}) collective-permute-start(bf16[1024,256]{1,0:T(8,128)(2,1)S(1)} %collective-permute-done.7), channel_id=1, source_target_pairs={{0,32},{8,40},{16,48},{24,56},{32,64},{40,72},{48,80},{56,88},{64,... | collective-permute-start | bytes 1572872 | tf_op jit(solution)/shard_map/ppermute | solution.py:291
  56.1 13.8 %collective-permute-start.5 = (bf16[1024,256]{1,0:T(8,128)(2,1)S(1)}, bf16[1024,256]{1,0:T(8,128)(2,1)S(1)}, u32[]{:S(2)}, u32[]{:S(2)}) collective-permute-start(bf16[1024,256]{1,0:T(8,128)(2,1)S(1)} %collective-permute-done.4), channel_id=1, source_target_pairs={{0,224},{8,232},{16,240},{24,248},{32,0},{40,8},{48,16},{56,24},{6... | collective-permute-start | bytes 1572872 | tf_op jit(solution)/shard_map/ppermute | solution.py:291
  59.8 19.0 %copy-start.5 = (bf16[576,256]{1,0:T(8,128)(2,1)}, bf16[576,256]{1,0:T(8,128)(2,1)S(1)}, u32[]{:S(2)}) copy-start(bf16[576,256]{1,0:T(8,128)(2,1)S(1)} %convolution_convert_fusion.refs_6_) | copy-start | bytes 884740
  69.8 7.7 %collective-permute-start.10 = (bf16[512,256]{1,0:T(8,128)(2,1)S(1)}, bf16[512,256]{1,0:T(8,128)(2,1)S(1)}, u32[]{:S(2)}, u32[]{:S(2)}) collective-permute-start(bf16[512,256]{1,0:T(8,128)(2,1)S(1)} %slice.55), channel_id=1, source_target_pairs={{0,32},{8,40},{16,48},{24,56},{32,64},{40,72},{48,80},{56,88},{64,... | collective-permute-start | bytes 786440 | tf_op jit(solution)/shard_map/ppermute | solution.py:291
  69.9 7.9 %collective-permute-start.9 = (bf16[512,256]{1,0:T(8,128)(2,1)S(1)}, bf16[512,256]{1,0:T(8,128)(2,1)S(1)}, u32[]{:S(2)}, u32[]{:S(2)}) collective-permute-start(bf16[512,256]{1,0:T(8,128)(2,1)S(1)} %slice.53), channel_id=1, source_target_pairs={{0,224},{8,232},{16,240},{24,248},{32,0},{40,8},{48,16},{56,24},{6... | collective-permute-start | bytes 786440 | tf_op jit(solution)/shard_map/ppermute | solution.py:291
  78.8 10.7 %copy-start.6 = (bf16[576,256]{1,0:T(8,128)(2,1)S(1)}, bf16[576,256]{1,0:T(8,128)(2,1)}, u32[]{:S(2)}) copy-start(bf16[576,256]{1,0:T(8,128)(2,1)} %convolution_convert_fusion.3.refs_2_) | copy-start | bytes 884740
  78.9 10.7 %copy-start.8 = (bf16[576,256]{1,0:T(8,128)(2,1)S(1)}, bf16[576,256]{1,0:T(8,128)(2,1)}, u32[]{:S(2)}) copy-start(bf16[576,256]{1,0:T(8,128)(2,1)} %convolution_convert_fusion.4.refs_3_) | copy-start | bytes 884740
  80.6 9.1 %copy-start.1 = (bf16[576,256]{1,0:T(8,128)(2,1)S(1)}, bf16[576,256]{1,0:T(8,128)(2,1)}, u32[]{:S(2)}) copy-start(bf16[576,256]{1,0:T(8,128)(2,1)} %fusion.refs_4_) | copy-start | bytes 884740
  80.6 9.1 %copy-start.7 = (bf16[576,256]{1,0:T(8,128)(2,1)S(1)}, bf16[576,256]{1,0:T(8,128)(2,1)}, u32[]{:S(2)}) copy-start(bf16[576,256]{1,0:T(8,128)(2,1)} %convolution_convert_fusion.2.refs_5_) | copy-start | bytes 884740
  80.6 16.4 %all-to-all-start = ((bf16[32,16,256]{2,1,0:T(8,128)(2,1)}), bf16[32,16,256]{2,1,0:T(8,128)(2,1)S(1)}, u32[]{:S(2)}, u32[]{:S(2)}) async-start(bf16[32,16,256]{2,1,0:T(8,128)(2,1)} %spread.1), calls=%async_computation | async-start | bytes 524288 | tf_op jit(solution)/shard_map/all_to_all | solution.py:370
  100.1 7.8 %copy-start.12 = (bf16[1,512,256]{2,1,0:T(8,128)(2,1)S(1)}, bf16[1,512,256]{2,1,0:T(8,128)(2,1)}, u32[]{:S(2)}) copy-start(bf16[1,512,256]{2,1,0:T(8,128)(2,1)} %fusion.5) | copy-start | bytes 786436
  100.1 43.5 %all-to-all-start.1 = ((bf16[32,16,1024]{2,1,0:T(8,128)(2,1)}), bf16[32,16,1024]{2,1,0:T(8,128)(2,1)S(1)}, u32[]{:S(2)}, u32[]{:S(2)}) async-start(bf16[32,16,1024]{2,1,0:T(8,128)(2,1)} %accepted_tile.1), calls=%async_computation.1 | async-start | bytes 2097152 | tf_op jit(solution)/shard_map/all_to_all | solution.py:372
  108.1 2.7 %collective-permute-start.11 = (bf16[4,512,256]{2,1,0:T(8,128)(2,1)S(1)}, bf16[4,512,256]{2,1,0:T(8,128)(2,1)S(1)}, u32[]{:S(2)}, u32[]{:S(2)}) collective-permute-start(bf16[4,512,256]{2,1,0:T(8,128)(2,1)S(1)} %pad_maximum_fusion), channel_id=1, source_target_pairs={{0,1},{1,0},{2,3},{3,2},{4,5},{5,4},{6,7},{7,6},{8,9},{9,8},{10,11... | collective-permute-start | bytes 3145736 | tf_op jit(solution)/shard_map/ppermute | solution.py:305
  115.2 9.4 %collective-permute-start.14 = (bf16[512,256]{1,0:T(8,128)(2,1)}, bf16[512,256]{1,0:T(8,128)(2,1)S(1)}, u32[]{:S(2)}, u32[]{:S(2)}) collective-permute-start(bf16[512,256]{1,0:T(8,128)(2,1)} %get-tuple-element.17), channel_id=1, source_target_pairs={{0,6},{1,7},{2,0},{3,1},{4,2},{5,3},{6,4},{7,5},{8,14},{9,15},{10,... | collective-permute-start | bytes 786440 | tf_op jit(solution)/shard_map/ppermute | solution.py:301
  116.8 10.9 %collective-permute-start.13 = (bf16[512,256]{1,0:T(8,128)(2,1)}, bf16[512,256]{1,0:T(8,128)(2,1)S(1)}, u32[]{:S(2)}, u32[]{:S(2)}) collective-permute-start(bf16[512,256]{1,0:T(8,128)(2,1)} %get-tuple-element.16), channel_id=1, source_target_pairs={{0,4},{1,5},{2,6},{3,7},{4,0},{5,1},{6,2},{7,3},{8,12},{9,13},{10,... | collective-permute-start | bytes 786440 | tf_op jit(solution)/shard_map/ppermute | solution.py:301
  118.0 14.1 %collective-permute-start.12 = (bf16[512,256]{1,0:T(8,128)(2,1)}, bf16[512,256]{1,0:T(8,128)(2,1)S(1)}, u32[]{:S(2)}, u32[]{:S(2)}) collective-permute-start(bf16[512,256]{1,0:T(8,128)(2,1)} %get-tuple-element.15), channel_id=1, source_target_pairs={{0,2},{1,3},{2,4},{3,5},{4,6},{5,7},{6,0},{7,1},{8,10},{9,11},{10,... | collective-permute-start | bytes 786440 | tf_op jit(solution)/shard_map/ppermute | solution.py:301
  134.0 5.3 %collective-permute-start.15 = (bf16[128,256]{1,0:T(8,128)(2,1)S(1)}, bf16[128,256]{1,0:T(8,128)(2,1)S(1)}, u32[]{:S(2)}, u32[]{:S(2)}) collective-permute-start(bf16[128,256]{1,0:T(8,128)(2,1)S(1)} %get-tuple-element.20), channel_id=1, source_target_pairs={{0,24},{8,0},{16,8},{24,16},{32,56},{40,32},{48,40},{56,48},{64,88... | collective-permute-start | bytes 196616 | tf_op jit(solution)/shard_map/ppermute | solution.py:296
  134.2 6.1 %collective-permute-start.16 = (bf16[128,256]{1,0:T(8,128)(2,1)S(1)}, bf16[128,256]{1,0:T(8,128)(2,1)S(1)}, u32[]{:S(2)}, u32[]{:S(2)}) collective-permute-start(bf16[128,256]{1,0:T(8,128)(2,1)S(1)} %get-tuple-element.19), channel_id=1, source_target_pairs={{0,16},{8,24},{16,0},{24,8},{32,48},{40,56},{48,32},{56,40},{64,80... | collective-permute-start | bytes 196616 | tf_op jit(solution)/shard_map/ppermute | solution.py:296
  136.9 4.3 %collective-permute-start.17 = (bf16[128,256]{1,0:T(8,128)(2,1)S(1)}, bf16[128,256]{1,0:T(8,128)(2,1)S(1)}, u32[]{:S(2)}, u32[]{:S(2)}) collective-permute-start(bf16[128,256]{1,0:T(8,128)(2,1)S(1)} %get-tuple-element.18), channel_id=1, source_target_pairs={{0,8},{8,16},{16,24},{24,0},{32,40},{40,48},{48,56},{56,32},{64,72... | collective-permute-start | bytes 196616 | tf_op jit(solution)/shard_map/ppermute | solution.py:296
  (9 other events, 16.9 us)

commit v2 on v1

--- a/solution.py
+++ b/solution.py
@@ -14,7 +14,7 @@
 GROUP = HEADS // KV_HEADS
 NODES, ACC = 64, 8
 Z, Y, X, C = 8, 4, 4, 2
-KEY_BLOCK = 1024
+KEY_BLOCK = 2048
 neg_large = -1e30
 
 
@@ -30,7 +30,7 @@
     *rest,
     request,
 ):
-    out_ref, picked_ref, scores, acc = rest[-4:]
+    *earlier, out_ref, scores, acc = rest
     nodes = q_ref.shape[0]
     rows = nodes * GROUP
     f32, bf16 = jnp.float32, jnp.bfloat16
@@ -86,21 +86,27 @@
     accepted = accepted_ref[request : request + 1, :]
     hot = lax.broadcasted_iota(jnp.int32, (nodes, accepted.shape[1]), 0) == accepted
     hot = hot.astype(f32).astype(bf16)
+    mine = slice(request * nodes, (request + 1) * nodes)
+    start = out_ref.shape[0] // (nodes + accepted.shape[1]) * nodes
+    start = start + request * accepted.shape[1]
+    for past in earlier:
+        out_ref[...] = past[...]
     for g in range(GROUP):
         one = attended[g * nodes : (g + 1) * nodes]
-        out_ref[:, g * HD : (g + 1) * HD] = one
-        picked_ref[:, g * HD : (g + 1) * HD] = lax.dot_general(
+        columns = slice(g * HD, (g + 1) * HD)
+        out_ref[mine, columns] = one
+        out_ref[start : start + accepted.shape[1], columns] = lax.dot_general(
             hot, one, first, preferred_element_type=f32
-        ).astype(picked_ref.dtype)
+        ).astype(out_ref.dtype)
 
 
 def attention(request, earlier, inputs):
     _, parents, queries, _, _, cache_keys, _, accepted_nodes = inputs
-    nodes = parents.shape[1]
+    requests, nodes = parents.shape
     cache = cache_keys.shape[1]
     rows = nodes * GROUP
-    count = accepted_nodes.shape[1]
     width = queries.shape[1]
+    packed = (requests * (nodes + accepted_nodes.shape[1]), width)
     per_node = lambda size: pl.BlockSpec((nodes, size), lambda i, lens: (request, 0))
     per_cache = pl.BlockSpec((1, cache, HD), lambda i, lens: (request, 0, 0))
     whole = lambda array: pl.BlockSpec(array.shape, lambda i, lens: (0, 0))
@@ -118,21 +124,14 @@
                 per_cache,
                 whole(accepted_nodes),
             ]
-            + [pl.BlockSpec(memory_space=pl.ANY)] * len(earlier),
-            out_specs=[
-                per_node(width),
-                pl.BlockSpec((count, width), lambda i, lens: (0, 0)),
-            ],
+            + [whole(array) for array in earlier],
+            out_specs=pl.BlockSpec(packed, lambda i, lens: (0, 0)),
             scratch_shapes=[
                 pltpu.VMEM((cache // KEY_BLOCK, KEY_BLOCK, rows), jnp.float32),
                 pltpu.VMEM((HD, rows), jnp.float32),
             ],
         ),
-        out_shape=[
-            jax.ShapeDtypeStruct(queries.shape, jnp.bfloat16),
-            jax.ShapeDtypeStruct((count, width), jnp.bfloat16),
-        ],
-        input_output_aliases={len(inputs): 0} if earlier else {},
+        out_shape=jax.ShapeDtypeStruct(packed, jnp.bfloat16),
         compiler_params=pltpu.CompilerParams(vmem_limit_bytes=62 * 1024 * 1024),
         cost_estimate=pl.CostEstimate(
             flops=rows * cache * HD * 8,
@@ -220,16 +219,16 @@
     )(*pieces)
 
 
-def spread_kernel(at_ref, *refs):
+def spread_kernel(z_ref, y_ref, *refs):
     blocks, out_ref = refs[:Z], refs[Z]
     count = out_ref.shape[1]
     for d, block in enumerate(blocks):
         for q in range(Y):
-            place = (at_ref[1] + Y - q) % Y * Z + (at_ref[0] + d) % Z
+            place = (y_ref[0] + Y - q) % Y * Z + (z_ref[0] + d) % Z
             out_ref[place] = block[q * count : (q + 1) * count, :]
 
 
-def spread(blocks, at):
+def spread(blocks, z, y):
     size, width = blocks[0].shape
     few = size * ACC // (NODES + ACC)
     count = few // Y
@@ -237,14 +236,36 @@
     return pl.pallas_call(
         spread_kernel,
         grid=(1,),
-        in_specs=[pl.BlockSpec(memory_space=pltpu.SMEM)] + [last] * Z,
+        in_specs=[pl.BlockSpec(memory_space=pltpu.SMEM)] * 2 + [last] * Z,
         out_specs=pl.BlockSpec((Y * Z, count, width), lambda i: (0, 0, 0)),
         out_shape=jax.ShapeDtypeStruct((Y * Z, count, width), blocks[0].dtype),
         cost_estimate=pl.CostEstimate(
             flops=count * width, bytes_accessed=Z * Y * count * width * 4, transcendentals=0
         ),
         name="spread",
-    )(at, *blocks)
+    )(z, y, *blocks)
+
+
+def place_kernel(y_ref, *refs):
+    parts, out_ref = refs[:Y], refs[Y]
+    for q, part in enumerate(parts):
+        for z in range(Z):
+            out_ref[z, (y_ref[0] + Y - q) % Y] = part[z]
+
+
+def place_accepted(parts, y):
+    _, count, width = parts[0].shape
+    return pl.pallas_call(
+        place_kernel,
+        in_specs=[pl.BlockSpec(memory_space=pltpu.SMEM)]
+        + [pl.BlockSpec(memory_space=pltpu.VMEM)] * Y,
+        out_specs=pl.BlockSpec(memory_space=pltpu.VMEM),
+        out_shape=jax.ShapeDtypeStruct((Z, Y, count, width), parts[0].dtype),
+        cost_estimate=pl.CostEstimate(
+            flops=parts[0].size, bytes_accessed=parts[0].size * 16, transcendentals=0
+        ),
+        name="place_accepted",
+    )(y, *parts)
 
 
 def tile_kernel(accepted_ref, residual_ref, parts_ref, out_ref):
@@ -343,12 +364,10 @@
         cache_values,
         accepted_nodes,
     )
-    earlier, picks = (), []
+    earlier = ()
     for r in range(requests):
-        attended, picked = attention(r, earlier, inputs)
-        earlier = (attended,)
-        picks.append(picked)
-    packed = jnp.concatenate([attended, *picks], axis=0)
+        packed = attention(r, earlier, inputs)
+        earlier = (packed,)
     packed = [packed] + [shift_y(packed, q) for q in range(1, Y)]
     gathered = gather_rows(packed)
 
@@ -363,14 +382,16 @@
     blocks = []
     for d in range(Z):
         blocks.append(partial(gathered, d))
-    few = spread(blocks, jnp.stack([z, y]))
+    few = spread(blocks, z[None], y[None])
     planes = [
         [device(zz, yy, j) for yy in range(Y) for j in range(X * C)] for zz in range(Z)
     ]
     few = lax.all_to_all(few, ("dp", "mp"), 0, 0, axis_index_groups=planes, tiled=True)
-    tiles = accepted_tile(residual, accepted_nodes, few, Z * Y)
-    accepted_hidden = lax.all_to_all(tiles, "dp", 0, 0, tiled=True)
-    accepted_hidden = accepted_hidden.reshape(Z * Y * count, Y * width)
+    tiles = accepted_tile(residual, accepted_nodes, few, Z)
+    along_z = [[zz * Y + yy for zz in range(Z)] for yy in range(Y)]
+    tiles = lax.all_to_all(tiles, "dp", 0, 0, axis_index_groups=along_z, tiled=True)
+    tiles = [tiles] + [shift_y(tiles, q) for q in range(1, Y)]
+    accepted_hidden = place_accepted(tiles, y[None]).reshape(Z * Y * count, Y * width)
 
     odd = (z + c) % 2
     come = swap_core(

time: 147 us -> 141 us (0.959)
  the two profiles are of different devices: /device:TPU:8 before, /device:TPU:2 now
where the time goes in v2:
time: 141 us
  waiting for transfers between devices  42.4 us (30%)
  starting transfers between devices  38.8 us (28%)
  Pallas kernels  28.7 us (20%)
  blocking collectives  16.1 us (11%)
  local copies, waits for them, and re-layouts  5.92 us (4%)
  matrix products  5.29 us (4%)
  other arithmetic  2.53 us (2%)
    ppermute x8, waiting for transfers between devices, shift_z(): return lax.ppermute(value, 'dp', pairs)  22 us
    ppermute x8, starting transfers between devices, shift_z(): return lax.ppermute(value, 'dp', pairs)  16.9 us
    all_to_all x1, blocking collectives, per_device(): lax.all_to_all(few, ('dp', 'mp'), 0, 0, axis_index_groups=planes, tiled=T...  16.1 us
    pallas_call x2, Pallas kernels, attention(): pl.pallas_call(functools.partial(attention_kernel, request=request), grid...  15.4 us
    ppermute x9, waiting for transfers between devices, shift_y(): return lax.ppermute(value, 'dp', pairs)  12.2 us
    ppermute x9, starting transfers between devices, shift_y(): return lax.ppermute(value, 'dp', pairs)  10.9 us
    all_to_all x1, starting transfers between devices, per_device(): lax.all_to_all(tiles, 'dp', 0, 0, axis_index_groups=along_z, tiled=True)  6.75 us
    unnamed x42, local copies, waits for them, and re-layouts  5.25 us
  transfers between devices with their start and end apart: 22, of which 11 were waited for; matrix products, arithmetic and copies ran while one was open for 6% of the time, Pallas kernels for 8%

profile of v2, /device:TPU:2, one launch (start us, length us, event | category | flops | bytes accessed | tf_op | source)
XLA Modules:
  0.0 140.7 jit_solution(12836832990433996604)
XLA Ops:
  0.6 7.6 %attention.2.rest_0_ = bf16[144,1024]{1,0:T(8,128)(2,1)} custom-call(s32[2]{0:T(128)} %lens_ref.3, s32[2,64]{1,0:T(2,128)} %parents_ref.3, bf16[128,1024]{1,0:T(8,128)(2,1)} %q_ref.3, bf16[128,128]{1,0:T(8,128)(2,1)} %tk_ref.3, bf16[128,128]{1,0:T(8,128)(2,1)} %tv_ref.3, bf16[2,4096,128]{2,1,0:T(8,128)(2,1)} %k_ref.3, bf16[2,4096,128]{2,1,0:T(8,128)(2,1)} %v_ref.3, ...), custom_call_target="tpu_custom_call" | custom-call | flops 2147483648 | bytes 2097152 | tf_op jit(solution)/shard_map/attention/pallas_call | solution.py:113
  8.2 7.8 %attention.3.refs_0_ = bf16[144,1024]{1,0:T(8,128)(2,1)} custom-call(s32[2]{0:T(128)} %lens_ref.3, s32[2,64]{1,0:T(2,128)} %parents_ref.3, bf16[128,1024]{1,0:T(8,128)(2,1)} %q_ref.3, bf16[128,128]{1,0:T(8,128)(2,1)} %tk_ref.3, bf16[128,128]{1,0:T(8,128)(2,1)} %tv_ref.3, bf16[2,4096,128]{2,1,0:T(8,128)(2,1)} %k_ref.3, bf16[2,4096,128]{2,1,0:T(8,128)(2,1)} %v_ref.3, ...), custom_call_target="tpu_custom_call" | custom-call | flops 2147483648 | bytes 2097152 | tf_op jit(solution)/shard_map/attention/pallas_call | solution.py:113
  16.0 1.6 %collective-permute-start = (bf16[144,1024]{1,0:T(8,128)(2,1)}, bf16[144,1024]{1,0:T(8,128)(2,1)S(1)}, u32[]{:S(2)}, u32[]{:S(2)}) collective-permute-start(bf16[144,1024]{1,0:T(8,128)(2,1)} %attention.3.refs_0_), channel_id=1, source_target_pairs={{0,8},{8,16},{16,24},{24,0},{32,40},{40,48},{48,56},{56,32},{64,72... | collective-permute-start | bytes 884744 | tf_op jit(solution)/shard_map/ppermute | solution.py:317
  17.6 2.9 %collective-permute-start.1 = (bf16[144,1024]{1,0:T(8,128)(2,1)}, bf16[144,1024]{1,0:T(8,128)(2,1)S(1)}, u32[]{:S(2)}, u32[]{:S(2)}) collective-permute-start(bf16[144,1024]{1,0:T(8,128)(2,1)} %attention.3.refs_0_), channel_id=1, source_target_pairs={{0,16},{8,24},{16,0},{24,8},{32,48},{40,56},{48,32},{56,40},{64,80... | collective-permute-start | bytes 884744 | tf_op jit(solution)/shard_map/ppermute | solution.py:317
  20.5 3.3 %collective-permute-start.6 = (bf16[1024,256]{1,0:T(8,128)(2,1)S(1)}, bf16[1024,256]{1,0:T(8,128)(2,1)S(1)}, u32[]{:S(2)}, u32[]{:S(2)}) collective-permute-start(bf16[1024,256]{1,0:T(8,128)(2,1)S(1)} %copy-done.20), channel_id=1, source_target_pairs={{0,32},{8,40},{16,48},{24,56},{32,64},{40,72},{48,80},{56,88},{64,... | collective-permute-start | bytes 1572872 | tf_op jit(solution)/shard_map/ppermute | solution.py:312
  23.8 2.4 %collective-permute-start.3 = (bf16[1024,256]{1,0:T(8,128)(2,1)S(1)}, bf16[1024,256]{1,0:T(8,128)(2,1)S(1)}, u32[]{:S(2)}, u32[]{:S(2)}) collective-permute-start(bf16[1024,256]{1,0:T(8,128)(2,1)S(1)} %copy-done.20), channel_id=1, source_target_pairs={{0,224},{8,232},{16,240},{24,248},{32,0},{40,8},{48,16},{56,24},{6... | collective-permute-start | bytes 1572872 | tf_op jit(solution)/shard_map/ppermute | solution.py:312
  26.2 7.5 %collective-permute-done.1.refs_2_ = bf16[144,1024]{1,0:T(8,128)(2,1)S(1)} collective-permute-done((bf16[144,1024]{1,0:T(8,128)(2,1)}, bf16[144,1024]{1,0:T(8,128)(2,1)S(1)}, u32[]{:S(2)}, u32[]{:S(2)}) %collective-permute-start.1) | collective-permute-done | bytes 294944 | tf_op jit(solution)/shard_map/ppermute | solution.py:317
  35.1 2.4 %gather_rows.1 = bf16[576,1024]{1,0:T(8,128)(2,1)} custom-call(bf16[144,1024]{1,0:T(8,128)(2,1)} %attention.3.refs_0_, bf16[144,1024]{1,0:T(8,128)(2,1)} %copy-done.11, bf16[144,1024]{1,0:T(8,128)(2,1)} %copy-done.12, bf16[144,1024]{1,0:T(8,128)(2,1)} %copy-done.13), custom_call_target="tpu_custom_call" | custom-call | flops 589824 | bytes 2359296 | tf_op jit(solution)/shard_map/gather_rows/pallas_call | solution.py:210
  37.5 1.8 %convolution_convert_fusion.5.refs_0_ = bf16[576,256]{1,0:T(8,128)(2,1)S(1)} fusion(bf16[576,1024]{1,0:T(8,128)(2,1)} %gather_rows.1, bf16[1024,256]{1,0:T(8,128)(2,1)S(1)} %copy-done.20), kind=kOutput, calls=%fused_computation.7 | convolution fusion | flops 302137344 | bytes 1998848 | tf_op jit(solution)/shard_map/dot_general | solution.py:376
  39.4 2.0 %collective-permute-start.7 = (bf16[1024,256]{1,0:T(8,128)(2,1)S(1)}, bf16[1024,256]{1,0:T(8,128)(2,1)S(1)}, u32[]{:S(2)}, u32[]{:S(2)}) collective-permute-start(bf16[1024,256]{1,0:T(8,128)(2,1)S(1)} %collective-permute-done.6), channel_id=1, source_target_pairs={{0,32},{8,40},{16,48},{24,56},{32,64},{40,72},{48,80},{56,88},{64,... | collective-permute-start | bytes 1572872 | tf_op jit(solution)/shard_map/ppermute | solution.py:312
  41.4 2.5 %collective-permute-start.4 = (bf16[1024,256]{1,0:T(8,128)(2,1)S(1)}, bf16[1024,256]{1,0:T(8,128)(2,1)S(1)}, u32[]{:S(2)}, u32[]{:S(2)}) collective-permute-start(bf16[1024,256]{1,0:T(8,128)(2,1)S(1)} %collective-permute-done.3), channel_id=1, source_target_pairs={{0,224},{8,232},{16,240},{24,248},{32,0},{40,8},{48,16},{56,24},{6... | collective-permute-start | bytes 1572872 | tf_op jit(solution)/shard_map/ppermute | solution.py:312
  45.0 9.8 %collective-permute-done.7 = bf16[1024,256]{1,0:T(8,128)(2,1)S(1)} collective-permute-done((bf16[1024,256]{1,0:T(8,128)(2,1)S(1)}, bf16[1024,256]{1,0:T(8,128)(2,1)S(1)}, u32[]{:S(2)}, u32[]{:S(2)}) %collective-permute-start.7) | collective-permute-done | bytes 524320 | tf_op jit(solution)/shard_map/ppermute | solution.py:312
  54.8 3.2 %collective-permute-start.5 = (bf16[1024,256]{1,0:T(8,128)(2,1)S(1)}, bf16[1024,256]{1,0:T(8,128)(2,1)S(1)}, u32[]{:S(2)}, u32[]{:S(2)}) collective-permute-start(bf16[1024,256]{1,0:T(8,128)(2,1)S(1)} %collective-permute-done.4), channel_id=1, source_target_pairs={{0,224},{8,232},{16,240},{24,248},{32,0},{40,8},{48,16},{56,24},{6... | collective-permute-start | bytes 1572872 | tf_op jit(solution)/shard_map/ppermute | solution.py:312
  59.2 9.0 %collective-permute-done.8 = bf16[1024,256]{1,0:T(8,128)(2,1)S(1)} collective-permute-done((bf16[1024,256]{1,0:T(8,128)(2,1)S(1)}, bf16[1024,256]{1,0:T(8,128)(2,1)S(1)}, u32[]{:S(2)}, u32[]{:S(2)}) %collective-permute-start.8) | collective-permute-done | bytes 524320 | tf_op jit(solution)/shard_map/ppermute | solution.py:312
  68.6 3.3 %collective-permute-start.9 = (bf16[512,256]{1,0:T(8,128)(2,1)S(1)}, bf16[512,256]{1,0:T(8,128)(2,1)S(1)}, u32[]{:S(2)}, u32[]{:S(2)}) collective-permute-start(bf16[512,256]{1,0:T(8,128)(2,1)S(1)} %slice.53), channel_id=1, source_target_pairs={{0,224},{8,232},{16,240},{24,248},{32,0},{40,8},{48,16},{56,24},{6... | collective-permute-start | bytes 786440 | tf_op jit(solution)/shard_map/ppermute | solution.py:312
  72.9 3.2 %collective-permute-done.10 = bf16[512,256]{1,0:T(8,128)(2,1)S(1)} collective-permute-done((bf16[512,256]{1,0:T(8,128)(2,1)S(1)}, bf16[512,256]{1,0:T(8,128)(2,1)S(1)}, u32[]{:S(2)}, u32[]{:S(2)}) %collective-permute-start.10) | collective-permute-done | bytes 262176 | tf_op jit(solution)/shard_map/ppermute | solution.py:312
  77.5 1.6 %spread.1 = bf16[32,16,256]{2,1,0:T(8,128)(2,1)} custom-call(s32[1]{0:T(128)} %bitcast.5.z_ref, s32[1]{0:T(128)} %bitcast.4.y_ref, bf16[576,256]{1,0:T(8,128)(2,1)} %copy-done.2, bf16[576,256]{1,0:T(8,128)(2,1)} %copy-done.3, bf16[576,256]{1,0:T(8,128)(2,1)} %copy-done.6, bf16[576,256]{1,0:T(8,128)(2,1)} %copy-done.8, bf16[576,256]{1,0:T(8,128)(2,1)} %copy-done.1, ...), custom_call_target="tpu_custom_call" | custom-call | flops 4096 | bytes 524288 | tf_op jit(solution)/shard_map/spread/pallas_call | solution.py:236
  79.1 16.1 %all_to_all.10.parts_ref = bf16[32,16,256]{2,1,0:T(8,128)(2,1)} all-to-all(bf16[32,16,256]{2,1,0:T(8,128)(2,1)} %spread.1), channel_id=1, replica_groups={{0,1,2,3,4,5,6,7,8,9,10,11,12,13,14,15,16,17,18,19,20,21,22,23,24,25,26..., dimensions={0} | all-to-all | bytes 524288 | tf_op jit(solution)/shard_map/all_to_all | solution.py:389
  95.2 2.0 %accepted_tile.1 = bf16[8,16,1024]{2,1,0:T(8,128)(2,1)} custom-call(s32[2,8]{1,0:T(2,128)} %accepted_ref.5, bf16[128,1024]{1,0:T(8,128)(2,1)} %residual_ref.3, bf16[32,16,256]{2,1,0:T(8,128)(2,1)} %all_to_all.10.parts_ref), custom_call_target="tpu_custom_call" | custom-call | flops 8388608 | bytes 1310720 | tf_op jit(solution)/shard_map/accepted_tile/pallas_call | solution.py:294
  97.2 6.8 %all-to-all-start.1 = ((bf16[8,16,1024]{2,1,0:T(8,128)(2,1)}), bf16[8,16,1024]{2,1,0:T(8,128)(2,1)S(1)}, u32[]{:S(2)}, u32[]{:S(2)}) async-start(bf16[8,16,1024]{2,1,0:T(8,128)(2,1)} %accepted_tile.1), calls=%async_computation.1 | async-start | bytes 524288 | tf_op jit(solution)/shard_map/all_to_all | solution.py:392
  105.4 3.3 %owner_sums.1 = (f32[512,256]{1,0:T(8,128)}, bf16[512,256]{1,0:T(8,128)(2,1)}, bf16[512,256]{1,0:T(8,128)(2,1)}, bf16[512,256]{1,0:T(8,128)(2,1)}) custom-call(s32[4]{0:T(128)} %fusion.9.want_ref, bf16[4,512,256]{2,1,0:T(8,128)(2,1)} %copy-done.10, bf16[576,256]{1,0:T(8,128)(2,1)} %copy-done.2, bf16[576,256]{1,0:T(8,128)(2,1)} %copy-done.3, ...), custom_call_target="tpu_custom_call" | custom-call | flops 589824 | bytes 3538944 | tf_op jit(solution)/shard_map/owner_sums/pallas_call | solution.py:183
  108.8 1.5 %collective-permute-start.14 = (bf16[512,256]{1,0:T(8,128)(2,1)}, bf16[512,256]{1,0:T(8,128)(2,1)S(1)}, u32[]{:S(2)}, u32[]{:S(2)}) collective-permute-start(bf16[512,256]{1,0:T(8,128)(2,1)} %get-tuple-element.9), channel_id=1, source_target_pairs={{0,6},{1,7},{2,0},{3,1},{4,2},{5,3},{6,4},{7,5},{8,14},{9,15},{10,... | collective-permute-start | bytes 786440 | tf_op jit(solution)/shard_map/ppermute | solution.py:322
  110.8 2.2 %collective-permute-start.12 = (bf16[512,256]{1,0:T(8,128)(2,1)}, bf16[512,256]{1,0:T(8,128)(2,1)S(1)}, u32[]{:S(2)}, u32[]{:S(2)}) collective-permute-start(bf16[512,256]{1,0:T(8,128)(2,1)} %get-tuple-element.7), channel_id=1, source_target_pairs={{0,2},{1,3},{2,4},{3,5},{4,6},{5,7},{6,0},{7,1},{8,10},{9,11},{10,... | collective-permute-start | bytes 786440 | tf_op jit(solution)/shard_map/ppermute | solution.py:322
  113.0 3.6 %all-to-all-done.1.refs_0_ = bf16[8,16,1024]{2,1,0:T(8,128)(2,1)S(1)} async-done(((bf16[8,16,1024]{2,1,0:T(8,128)(2,1)}), bf16[8,16,1024]{2,1,0:T(8,128)(2,1)S(1)}, u32[]{:S(2)}, u32[]{:S(2)}) %all-to-all-start.1) | async-done | bytes 262176 | tf_op jit(solution)/shard_map/all_to_all | solution.py:392
  117.2 2.0 %collective-permute-start.19 = (bf16[8,16,1024]{2,1,0:T(8,128)(2,1)S(1)}, bf16[8,16,1024]{2,1,0:T(8,128)(2,1)S(1)}, u32[]{:S(2)}, u32[]{:S(2)}) collective-permute-start(bf16[8,16,1024]{2,1,0:T(8,128)(2,1)S(1)} %all-to-all-done.1.refs_0_), channel_id=1, source_target_pairs={{0,16},{8,24},{16,0},{24,8},{32,48},{40,56},{48,32},{56,40},{64,80... | collective-permute-start | bytes 786440 | tf_op jit(solution)/shard_map/ppermute | solution.py:317
  119.2 3.9 %collective-permute-done.14 = bf16[512,256]{1,0:T(8,128)(2,1)S(1)} collective-permute-done((bf16[512,256]{1,0:T(8,128)(2,1)}, bf16[512,256]{1,0:T(8,128)(2,1)S(1)}, u32[]{:S(2)}, u32[]{:S(2)}) %collective-permute-start.14) | collective-permute-done | bytes 262176 | tf_op jit(solution)/shard_map/ppermute | solution.py:322
  124.9 1.2 add_convert_fusion
  127.8 1.5 %collective-permute-start.16 = (bf16[128,256]{1,0:T(8,128)(2,1)S(1)}, bf16[128,256]{1,0:T(8,128)(2,1)S(1)}, u32[]{:S(2)}, u32[]{:S(2)}) collective-permute-start(bf16[128,256]{1,0:T(8,128)(2,1)S(1)} %get-tuple-element.11), channel_id=1, source_target_pairs={{0,16},{8,24},{16,0},{24,8},{32,48},{40,56},{48,32},{56,40},{64,80... | collective-permute-start | bytes 196616 | tf_op jit(solution)/shard_map/ppermute | solution.py:317
  129.4 3.3 %collective-permute-done.18.refs_1_ = bf16[8,16,1024]{2,1,0:T(8,128)(2,1)S(1)} collective-permute-done((bf16[8,16,1024]{2,1,0:T(8,128)(2,1)S(1)}, bf16[8,16,1024]{2,1,0:T(8,128)(2,1)S(1)}, u32[]{:S(2)}, u32[]{:S(2)}) %collective-permute-start.18) | collective-permute-done | bytes 262176 | tf_op jit(solution)/shard_map/ppermute | solution.py:317
  134.8 2.2 %place_accepted.1 = bf16[8,4,16,1024]{3,2,1,0:T(8,128)(2,1)} custom-call(s32[1]{0:T(128)} %bitcast.4.y_ref, bf16[8,16,1024]{2,1,0:T(8,128)(2,1)} %copy-done.9, bf16[8,16,1024]{2,1,0:T(8,128)(2,1)} %copy-done.14, bf16[8,16,1024]{2,1,0:T(8,128)(2,1)} %copy-done.15, bf16[8,16,1024]{2,1,0:T(8,128)(2,1)} %copy-done.16), custom_call_target="tpu_custom_call" | custom-call | flops 131072 | bytes 2097152 | tf_op jit(solution)/shard_map/place_accepted/pallas_call | solution.py:258
  137.0 1.2 collective-permute-done.17.refs_3_
  138.8 1.8 %shard_map.113 = bf16[128,1024]{1,0:T(8,128)(2,1)} custom-call(s32[4]{0:T(128)} %and_select_fusion.1.place_ref, bf16[128,1024]{1,0:T(8,128)(2,1)} %residual_ref.3, bf16[128,256]{1,0:T(8,128)(2,1)} %get-tuple-element.13.refs_0_, bf16[128,256]{1,0:T(8,128)(2,1)} %copy-done.17, bf16[128,256]{1,0:T(8,128)(2,1)} %copy-done.18, bf16[128,256]{1,0:T(8,128)(2,1)} %copy-done.19), custom_call_target="tpu_custom_call" | custom-call | flops 131072 | bytes 524288 | tf_op jit(solution)/shard_map/pallas_call | solution.py:156
  (83 shorter events, 15.4 us)
Async XLA Ops:
  8.2 12.3 %copy-start.20 = (bf16[1024,256]{1,0:T(8,128)(2,1)S(1)}, bf16[1024,256]{1,0:T(8,128)(2,1)}, u32[]{:S(2)}) copy-start(bf16[1024,256]{1,0:T(8,128)(2,1)} %param.19) | copy-start | bytes 1572868
  16.0 10.2 %collective-permute-start = (bf16[144,1024]{1,0:T(8,128)(2,1)}, bf16[144,1024]{1,0:T(8,128)(2,1)S(1)}, u32[]{:S(2)}, u32[]{:S(2)}) collective-permute-start(bf16[144,1024]{1,0:T(8,128)(2,1)} %attention.3.refs_0_), channel_id=1, source_target_pairs={{0,8},{8,16},{16,24},{24,0},{32,40},{40,48},{48,56},{56,32},{64,72... | collective-permute-start | bytes 884744 | tf_op jit(solution)/shard_map/ppermute | solution.py:317
  17.6 16.1 %collective-permute-start.1 = (bf16[144,1024]{1,0:T(8,128)(2,1)}, bf16[144,1024]{1,0:T(8,128)(2,1)S(1)}, u32[]{:S(2)}, u32[]{:S(2)}) collective-permute-start(bf16[144,1024]{1,0:T(8,128)(2,1)} %attention.3.refs_0_), channel_id=1, source_target_pairs={{0,16},{8,24},{16,0},{24,8},{32,48},{40,56},{48,32},{56,40},{64,80... | collective-permute-start | bytes 884744 | tf_op jit(solution)/shard_map/ppermute | solution.py:317
  20.5 13.3 %collective-permute-start.2 = (bf16[144,1024]{1,0:T(8,128)(2,1)}, bf16[144,1024]{1,0:T(8,128)(2,1)S(1)}, u32[]{:S(2)}, u32[]{:S(2)}) collective-permute-start(bf16[144,1024]{1,0:T(8,128)(2,1)} %attention.3.refs_0_), channel_id=1, source_target_pairs={{0,24},{8,0},{16,8},{24,16},{32,56},{40,32},{48,40},{56,48},{64,88... | collective-permute-start | bytes 884744 | tf_op jit(solution)/shard_map/ppermute | solution.py:317
  20.5 18.9 %collective-permute-start.6 = (bf16[1024,256]{1,0:T(8,128)(2,1)S(1)}, bf16[1024,256]{1,0:T(8,128)(2,1)S(1)}, u32[]{:S(2)}, u32[]{:S(2)}) collective-permute-start(bf16[1024,256]{1,0:T(8,128)(2,1)S(1)} %copy-done.20), channel_id=1, source_target_pairs={{0,32},{8,40},{16,48},{24,56},{32,64},{40,72},{48,80},{56,88},{64,... | collective-permute-start | bytes 1572872 | tf_op jit(solution)/shard_map/ppermute | solution.py:312
  23.8 17.6 %collective-permute-start.3 = (bf16[1024,256]{1,0:T(8,128)(2,1)S(1)}, bf16[1024,256]{1,0:T(8,128)(2,1)S(1)}, u32[]{:S(2)}, u32[]{:S(2)}) collective-permute-start(bf16[1024,256]{1,0:T(8,128)(2,1)S(1)} %copy-done.20), channel_id=1, source_target_pairs={{0,224},{8,232},{16,240},{24,248},{32,0},{40,8},{48,16},{56,24},{6... | collective-permute-start | bytes 1572872 | tf_op jit(solution)/shard_map/ppermute | solution.py:312
  26.2 7.5 %copy-start.11 = (bf16[144,1024]{1,0:T(8,128)(2,1)}, bf16[144,1024]{1,0:T(8,128)(2,1)S(1)}, u32[]{:S(2)}) copy-start(bf16[144,1024]{1,0:T(8,128)(2,1)S(1)} %collective-permute-done.refs_1_) | copy-start | bytes 884740
  37.5 6.3 %copy-start = (bf16[576,1024]{1,0:T(8,128)(2,1)S(1)}, bf16[576,1024]{1,0:T(8,128)(2,1)}, u32[]{:S(2)}) copy-start(bf16[576,1024]{1,0:T(8,128)(2,1)} %gather_rows.1) | copy-start | bytes 3538948
  39.3 5.0 %copy-start.2 = (bf16[576,256]{1,0:T(8,128)(2,1)}, bf16[576,256]{1,0:T(8,128)(2,1)S(1)}, u32[]{:S(2)}) copy-start(bf16[576,256]{1,0:T(8,128)(2,1)S(1)} %convolution_convert_fusion.5.refs_0_) | copy-start | bytes 884740
  39.4 15.4 %collective-permute-start.7 = (bf16[1024,256]{1,0:T(8,128)(2,1)S(1)}, bf16[1024,256]{1,0:T(8,128)(2,1)S(1)}, u32[]{:S(2)}, u32[]{:S(2)}) collective-permute-start(bf16[1024,256]{1,0:T(8,128)(2,1)S(1)} %collective-permute-done.6), channel_id=1, source_target_pairs={{0,32},{8,40},{16,48},{24,56},{32,64},{40,72},{48,80},{56,88},{64,... | collective-permute-start | bytes 1572872 | tf_op jit(solution)/shard_map/ppermute | solution.py:312
  41.4 13.4 %collective-permute-start.4 = (bf16[1024,256]{1,0:T(8,128)(2,1)S(1)}, bf16[1024,256]{1,0:T(8,128)(2,1)S(1)}, u32[]{:S(2)}, u32[]{:S(2)}) collective-permute-start(bf16[1024,256]{1,0:T(8,128)(2,1)S(1)} %collective-permute-done.3), channel_id=1, source_target_pairs={{0,224},{8,232},{16,240},{24,248},{32,0},{40,8},{48,16},{56,24},{6... | collective-permute-start | bytes 1572872 | tf_op jit(solution)/shard_map/ppermute | solution.py:312
  45.0 13.5 %copy-start.4 = (bf16[576,256]{1,0:T(8,128)(2,1)}, bf16[576,256]{1,0:T(8,128)(2,1)S(1)}, u32[]{:S(2)}) copy-start(bf16[576,256]{1,0:T(8,128)(2,1)S(1)} %convolution_convert_fusion.1.refs_7_) | copy-start | bytes 884740
  54.8 13.4 %collective-permute-start.8 = (bf16[1024,256]{1,0:T(8,128)(2,1)S(1)}, bf16[1024,256]{1,0:T(8,128)(2,1)S(1)}, u32[]{:S(2)}, u32[]{:S(2)}) collective-permute-start(bf16[1024,256]{1,0:T(8,128)(2,1)S(1)} %collective-permute-done.7), channel_id=1, source_target_pairs={{0,32},{8,40},{16,48},{24,56},{32,64},{40,72},{48,80},{56,88},{64,... | collective-permute-start | bytes 1572872 | tf_op jit(solution)/shard_map/ppermute | solution.py:312
  54.8 13.7 %collective-permute-start.5 = (bf16[1024,256]{1,0:T(8,128)(2,1)S(1)}, bf16[1024,256]{1,0:T(8,128)(2,1)S(1)}, u32[]{:S(2)}, u32[]{:S(2)}) collective-permute-start(bf16[1024,256]{1,0:T(8,128)(2,1)S(1)} %collective-permute-done.4), channel_id=1, source_target_pairs={{0,224},{8,232},{16,240},{24,248},{32,0},{40,8},{48,16},{56,24},{6... | collective-permute-start | bytes 1572872 | tf_op jit(solution)/shard_map/ppermute | solution.py:312
  59.2 13.6 %copy-start.6 = (bf16[576,256]{1,0:T(8,128)(2,1)}, bf16[576,256]{1,0:T(8,128)(2,1)S(1)}, u32[]{:S(2)}) copy-start(bf16[576,256]{1,0:T(8,128)(2,1)S(1)} %convolution_convert_fusion.3.refs_2_) | copy-start | bytes 884740
  68.3 7.8 %collective-permute-start.10 = (bf16[512,256]{1,0:T(8,128)(2,1)S(1)}, bf16[512,256]{1,0:T(8,128)(2,1)S(1)}, u32[]{:S(2)}, u32[]{:S(2)}) collective-permute-start(bf16[512,256]{1,0:T(8,128)(2,1)S(1)} %slice.55), channel_id=1, source_target_pairs={{0,32},{8,40},{16,48},{24,56},{32,64},{40,72},{48,80},{56,88},{64,... | collective-permute-start | bytes 786440 | tf_op jit(solution)/shard_map/ppermute | solution.py:312
  68.6 7.9 %collective-permute-start.9 = (bf16[512,256]{1,0:T(8,128)(2,1)S(1)}, bf16[512,256]{1,0:T(8,128)(2,1)S(1)}, u32[]{:S(2)}, u32[]{:S(2)}) collective-permute-start(bf16[512,256]{1,0:T(8,128)(2,1)S(1)} %slice.53), channel_id=1, source_target_pairs={{0,224},{8,232},{16,240},{24,248},{32,0},{40,8},{48,16},{56,24},{6... | collective-permute-start | bytes 786440 | tf_op jit(solution)/shard_map/ppermute | solution.py:312
  72.3 4.4 %copy-start.7 = (bf16[576,256]{1,0:T(8,128)(2,1)}, bf16[576,256]{1,0:T(8,128)(2,1)S(1)}, u32[]{:S(2)}) copy-start(bf16[576,256]{1,0:T(8,128)(2,1)S(1)} %convolution_convert_fusion.2.refs_5_) | copy-start | bytes 884740
  72.8 3.9 %copy-start.8 = (bf16[576,256]{1,0:T(8,128)(2,1)}, bf16[576,256]{1,0:T(8,128)(2,1)S(1)}, u32[]{:S(2)}) copy-start(bf16[576,256]{1,0:T(8,128)(2,1)S(1)} %convolution_convert_fusion.4.refs_3_) | copy-start | bytes 884740
  77.5 27.0 %collective-permute-start.11 = (bf16[4,512,256]{2,1,0:T(8,128)(2,1)S(1)}, bf16[4,512,256]{2,1,0:T(8,128)(2,1)S(1)}, u32[]{:S(2)}, u32[]{:S(2)}) collective-permute-start(bf16[4,512,256]{2,1,0:T(8,128)(2,1)S(1)} %pad_maximum_fusion), channel_id=1, source_target_pairs={{0,1},{1,0},{2,3},{3,2},{4,5},{5,4},{6,7},{7,6},{8,9},{9,8},{10,11... | collective-permute-start | bytes 3145736 | tf_op jit(solution)/shard_map/ppermute | solution.py:326
  97.2 19.3 %all-to-all-start.1 = ((bf16[8,16,1024]{2,1,0:T(8,128)(2,1)}), bf16[8,16,1024]{2,1,0:T(8,128)(2,1)S(1)}, u32[]{:S(2)}, u32[]{:S(2)}) async-start(bf16[8,16,1024]{2,1,0:T(8,128)(2,1)} %accepted_tile.1), calls=%async_computation.1 | async-start | bytes 524288 | tf_op jit(solution)/shard_map/all_to_all | solution.py:392
  108.8 14.3 %collective-permute-start.14 = (bf16[512,256]{1,0:T(8,128)(2,1)}, bf16[512,256]{1,0:T(8,128)(2,1)S(1)}, u32[]{:S(2)}, u32[]{:S(2)}) collective-permute-start(bf16[512,256]{1,0:T(8,128)(2,1)} %get-tuple-element.9), channel_id=1, source_target_pairs={{0,6},{1,7},{2,0},{3,1},{4,2},{5,3},{6,4},{7,5},{8,14},{9,15},{10,... | collective-permute-start | bytes 786440 | tf_op jit(solution)/shard_map/ppermute | solution.py:322
  110.2 14.0 %collective-permute-start.13 = (bf16[512,256]{1,0:T(8,128)(2,1)}, bf16[512,256]{1,0:T(8,128)(2,1)S(1)}, u32[]{:S(2)}, u32[]{:S(2)}) collective-permute-start(bf16[512,256]{1,0:T(8,128)(2,1)} %get-tuple-element.8), channel_id=1, source_target_pairs={{0,4},{1,5},{2,6},{3,7},{4,0},{5,1},{6,2},{7,3},{8,12},{9,13},{10,... | collective-permute-start | bytes 786440 | tf_op jit(solution)/shard_map/ppermute | solution.py:322
  110.8 14.1 %collective-permute-start.12 = (bf16[512,256]{1,0:T(8,128)(2,1)}, bf16[512,256]{1,0:T(8,128)(2,1)S(1)}, u32[]{:S(2)}, u32[]{:S(2)}) collective-permute-start(bf16[512,256]{1,0:T(8,128)(2,1)} %get-tuple-element.7), channel_id=1, source_target_pairs={{0,2},{1,3},{2,4},{3,5},{4,6},{5,7},{6,0},{7,1},{8,10},{9,11},{10,... | collective-permute-start | bytes 786440 | tf_op jit(solution)/shard_map/ppermute | solution.py:322
  116.5 16.9 %copy-start.9 = (bf16[8,16,1024]{2,1,0:T(8,128)(2,1)}, bf16[8,16,1024]{2,1,0:T(8,128)(2,1)S(1)}, u32[]{:S(2)}) copy-start(bf16[8,16,1024]{2,1,0:T(8,128)(2,1)S(1)} %all-to-all-done.1.refs_0_) | copy-start | bytes 786436
  116.6 16.2 %collective-permute-start.18 = (bf16[8,16,1024]{2,1,0:T(8,128)(2,1)S(1)}, bf16[8,16,1024]{2,1,0:T(8,128)(2,1)S(1)}, u32[]{:S(2)}, u32[]{:S(2)}) collective-permute-start(bf16[8,16,1024]{2,1,0:T(8,128)(2,1)S(1)} %all-to-all-done.1.refs_0_), channel_id=1, source_target_pairs={{0,8},{8,16},{16,24},{24,0},{32,40},{40,48},{48,56},{56,32},{64,72... | collective-permute-start | bytes 786440 | tf_op jit(solution)/shard_map/ppermute | solution.py:317
  117.2 16.2 %collective-permute-start.19 = (bf16[8,16,1024]{2,1,0:T(8,128)(2,1)S(1)}, bf16[8,16,1024]{2,1,0:T(8,128)(2,1)S(1)}, u32[]{:S(2)}, u32[]{:S(2)}) collective-permute-start(bf16[8,16,1024]{2,1,0:T(8,128)(2,1)S(1)} %all-to-all-done.1.refs_0_), channel_id=1, source_target_pairs={{0,16},{8,24},{16,0},{24,8},{32,48},{40,56},{48,32},{56,40},{64,80... | collective-permute-start | bytes 786440 | tf_op jit(solution)/shard_map/ppermute | solution.py:317
  123.1 10.4 %collective-permute-start.20 = (bf16[8,16,1024]{2,1,0:T(8,128)(2,1)S(1)}, bf16[8,16,1024]{2,1,0:T(8,128)(2,1)S(1)}, u32[]{:S(2)}, u32[]{:S(2)}) collective-permute-start(bf16[8,16,1024]{2,1,0:T(8,128)(2,1)S(1)} %all-to-all-done.1.refs_0_), channel_id=1, source_target_pairs={{0,24},{8,0},{16,8},{24,16},{32,56},{40,32},{48,40},{56,48},{64,88... | collective-permute-start | bytes 786440 | tf_op jit(solution)/shard_map/ppermute | solution.py:317
  126.7 10.3 %collective-permute-start.15 = (bf16[128,256]{1,0:T(8,128)(2,1)S(1)}, bf16[128,256]{1,0:T(8,128)(2,1)S(1)}, u32[]{:S(2)}, u32[]{:S(2)}) collective-permute-start(bf16[128,256]{1,0:T(8,128)(2,1)S(1)} %get-tuple-element.12), channel_id=1, source_target_pairs={{0,24},{8,0},{16,8},{24,16},{32,56},{40,32},{48,40},{56,48},{64,88... | collective-permute-start | bytes 196616 | tf_op jit(solution)/shard_map/ppermute | solution.py:317
  127.8 9.2 %collective-permute-start.16 = (bf16[128,256]{1,0:T(8,128)(2,1)S(1)}, bf16[128,256]{1,0:T(8,128)(2,1)S(1)}, u32[]{:S(2)}, u32[]{:S(2)}) collective-permute-start(bf16[128,256]{1,0:T(8,128)(2,1)S(1)} %get-tuple-element.11), channel_id=1, source_target_pairs={{0,16},{8,24},{16,0},{24,8},{32,48},{40,56},{48,32},{56,40},{64,80... | collective-permute-start | bytes 196616 | tf_op jit(solution)/shard_map/ppermute | solution.py:317
  132.7 5.5 %collective-permute-start.17 = (bf16[128,256]{1,0:T(8,128)(2,1)S(1)}, bf16[128,256]{1,0:T(8,128)(2,1)S(1)}, u32[]{:S(2)}, u32[]{:S(2)}) collective-permute-start(bf16[128,256]{1,0:T(8,128)(2,1)S(1)} %get-tuple-element.10), channel_id=1, source_target_pairs={{0,8},{8,16},{16,24},{24,0},{32,40},{40,48},{48,56},{56,32},{64,72... | collective-permute-start | bytes 196616 | tf_op jit(solution)/shard_map/ppermute | solution.py:317
  137.0 1.2 copy-start.17
  (11 other events, 8.5 us)
